TPU v7x, 256 devices: a whole 4x4x8 slice. The times are simulated.
256 devices in a mesh: ep: 64 (over z, x, core), tp: 4 (over y).
Axes of the slice: x: 4, y: 4, z: 8, core: 2. Of those that a mesh axis runs over, the one named last changes fastest.
Arguments:
- hidden: bfloat16 [4096, 2880], P('ep'), may hold values from -0.59765625 to 0.59765625
- queries: bfloat16 [4096, 2048], P('ep', 'tp'), may hold values from -160 to 160
- new_keys: bfloat16 [4096, 256], P('ep', 'tp'), may hold values from -6 to 6
- new_values: bfloat16 [4096, 256], P('ep', 'tp'), may hold values from -6 to 6
- key_cache: bfloat16 [512, 4, 64, 1024], P('ep', 'tp'), may hold values from -6 to 6
- value_cache: bfloat16 [512, 4, 64, 1024], P('ep', 'tp'), may hold values from -6 to 6
- cache_lengths: int32 [512], P('ep'), may hold values from 16 to 1024
- w_out: bfloat16 [2048, 2880], P('tp'), may hold values from -0.125 to 0.125
- w_router: bfloat16 [2880, 64], replicated, may hold values from -0.109375 to 0.109375
- routes: int32 [4096, 4], P('ep'), may hold values from 0 to 63, all different within a row; in each aligned block of 16 rows (0 to 15, 16 to 31, ...) at most 2 rows name the same one
- w_gate: bfloat16 [64, 2880, 1536], P('ep', None, 'tp'), may hold values from -0.109375 to 0.109375
- w_up: bfloat16 [64, 2880, 1536], P('ep', None, 'tp'), may hold values from -0.109375 to 0.109375
- w_down: bfloat16 [64, 1536, 2880], P('ep', 'tp'), may hold values from -0.15625 to 0.15625
Outputs:
- layer_out: bfloat16 [4096, 2880], P(('ep', 'tp'))
Inputs may be any that keep to these rules, and one draw needn't show every extreme that they name: `routes`: each token names 4 different experts; in each aligned block of 16 tokens no expert is named by more than 2 tokens, and in some blocks one expert is named by exactly 2.
All inputs are finite; a program needn't handle non-finite values.
Results may differ from a plain program's by a relative error of at most 0.02.
Values may be sent and summed in bfloat16 or wider, within the bound.
A program may use at most 64 MiB of HBM per device.

v0:
```python
import jax
import jax.numpy as jnp
from jax import lax
from jax.sharding import PartitionSpec as P


def in_blocks(x, dim, peers):
    before, after = (x.shape[:dim], x.shape[dim + 1 :])
    return jnp.moveaxis(x.reshape(*before, peers, -1, *after), dim, 0)


def sent_and_summed(x, axis, dim):
    parts = in_blocks(x, dim, lax.axis_size(axis))
    arrived = lax.all_to_all(parts, axis, split_axis=0, concat_axis=0, tiled=True)
    return arrived.astype(jnp.float32).sum(axis=0)


def attend(queries, new_keys, new_values, key_cache, value_cache, cache_lengths):
    seq_count, kv_count, head_dim, length = key_cache.shape
    new_count = queries.shape[0] // seq_count
    group_size = queries.shape[1] // (kv_count * head_dim)
    row_count = new_count * group_size
    scale = head_dim ** (-0.5)
    query_block = queries.reshape(seq_count, new_count, kv_count, group_size, head_dim)
    query_block = query_block.transpose(0, 2, 1, 3, 4).reshape(
        seq_count, kv_count, row_count, head_dim
    )
    fresh_keys = new_keys.reshape(seq_count, new_count, kv_count, head_dim).transpose(0, 2, 1, 3)
    fresh_values = new_values.reshape(seq_count, new_count, kv_count, head_dim).transpose(
        0, 2, 1, 3
    )
    cache_scores = (
        jnp.einsum("skrd,skdl->skrl", query_block, key_cache, preferred_element_type=jnp.float32)
        * scale
    )
    in_cache = jnp.arange(length)[None, :] < cache_lengths[:, None]
    cache_scores = jnp.where(in_cache[:, None, None, :], cache_scores, -1e30)
    fresh_scores = (
        jnp.einsum("skrd,sknd->skrn", query_block, fresh_keys, preferred_element_type=jnp.float32)
        * scale
    )
    causal = (jnp.arange(row_count) // group_size)[:, None] >= jnp.arange(new_count)[None, :]
    fresh_scores = jnp.where(causal[None, None, :, :], fresh_scores, -1e30)
    row_max = jnp.maximum(
        jnp.max(cache_scores, -1, keepdims=True), jnp.max(fresh_scores, -1, keepdims=True)
    )
    cache_exp = jnp.exp(cache_scores - row_max)
    fresh_exp = jnp.exp(fresh_scores - row_max)
    denom_sum = jnp.sum(cache_exp, -1, keepdims=True) + jnp.sum(fresh_exp, -1, keepdims=True)
    cache_probs = (cache_exp / denom_sum).astype(jnp.bfloat16)
    fresh_probs = (fresh_exp / denom_sum).astype(jnp.bfloat16)
    head_mix = jnp.einsum(
        "skrl,skdl->skrd", cache_probs, value_cache, preferred_element_type=jnp.float32
    )
    head_mix = head_mix + jnp.einsum(
        "skrn,sknd->skrd", fresh_probs, fresh_values, preferred_element_type=jnp.float32
    )
    head_mix = head_mix.reshape(seq_count, kv_count, new_count, group_size, head_dim).transpose(
        0, 2, 1, 3, 4
    )
    return head_mix.reshape(seq_count * new_count, kv_count * group_size * head_dim).astype(
        jnp.bfloat16
    )


def expert_apply(received, w_gate, w_up, w_down):
    width = received.shape[-1]
    flat_rows = received.reshape(-1, width)
    gate_proj = jnp.dot(flat_rows, w_gate[0], preferred_element_type=jnp.float32)
    up_proj = jnp.dot(flat_rows, w_up[0], preferred_element_type=jnp.float32)
    activated = ((up_proj + 1.0) * gate_proj * jax.nn.sigmoid(1.702 * gate_proj)).astype(
        jnp.bfloat16
    )
    partial_out = jnp.dot(activated, w_down[0], preferred_element_type=jnp.float32)
    return partial_out.reshape(received.shape[0], received.shape[1], width)


def body(
    hidden,
    queries,
    new_keys,
    new_values,
    key_cache,
    value_cache,
    cache_lengths,
    w_out,
    w_router,
    routes,
    w_gate,
    w_up,
    w_down,
):
    tp_size = lax.axis_size("tp")
    tp_index = lax.axis_index("tp")
    width = hidden.shape[1]
    block_rows = hidden.shape[0] // tp_size
    top_count = routes.shape[1]
    experts = w_router.shape[1]
    capacity = min(block_rows, max(2, (2 * block_rows * top_count + experts - 1) // experts))
    start_row = tp_index * block_rows
    attended = attend(queries, new_keys, new_values, key_cache, value_cache, cache_lengths)
    partial_value = jnp.dot(attended, w_out, preferred_element_type=jnp.float32)
    summed = sent_and_summed(partial_value.astype(jnp.bfloat16), "tp", 0)
    residual = (
        lax.dynamic_slice_in_dim(hidden, start_row, block_rows, 0).astype(jnp.float32) + summed
    )
    local_routes = lax.dynamic_slice_in_dim(routes, start_row, block_rows, 0)
    block_count = 1
    normed = (
        residual * lax.rsqrt(jnp.mean(residual * residual, -1, keepdims=True) + 1e-05)
    ).astype(jnp.bfloat16)
    logits = jnp.dot(normed, w_router, preferred_element_type=jnp.float32)
    expert_ids = jnp.arange(experts, dtype=jnp.int32)
    matches = local_routes[:, :, None] == expert_ids[None, None, :]
    picked = jnp.sum(jnp.where(matches, logits[:, None, :], 0.0), -1)
    picked_exp = jnp.exp(picked)
    weights = picked_exp / jnp.sum(picked_exp, -1, keepdims=True)
    flat_routes = local_routes.reshape(-1)
    one_hot = (
        flat_routes.reshape(block_count, block_rows * top_count)[:, :, None]
        == expert_ids[None, None, :]
    ).astype(jnp.int32)
    slot_rank = jnp.sum((jnp.cumsum(one_hot, 1) - one_hot) * one_hot, -1)
    slot_index = (
        slot_rank + (jnp.arange(block_count, dtype=jnp.int32) * capacity)[:, None]
    ).reshape(-1)
    outgoing = jnp.zeros((experts, block_count * capacity, width), jnp.bfloat16)
    outgoing = outgoing.at[flat_routes, slot_index].set(jnp.repeat(normed, top_count, axis=0))
    grouped = expert_apply(
        lax.all_gather(
            lax.all_to_all(outgoing, "ep", split_axis=0, concat_axis=0, tiled=True),
            "tp",
            axis=1,
            tiled=True,
        ),
        w_gate,
        w_up,
        w_down,
    )
    group_total = lax.psum_scatter(
        grouped.astype(jnp.bfloat16), "tp", scatter_dimension=1, tiled=True
    ).astype(jnp.float32)
    returned = lax.all_to_all(
        group_total.astype(jnp.bfloat16), "ep", split_axis=0, concat_axis=0, tiled=True
    ).astype(group_total.dtype)
    routed = returned[flat_routes, slot_index].reshape(-1, top_count, width)
    mixture = jnp.sum(weights[:, :, None] * routed, 1)
    return (residual + mixture).astype(jnp.bfloat16)


def solution(mesh):
    return jax.shard_map(
        body,
        mesh=mesh,
        in_specs=(
            P("ep", None),
            P("ep", "tp"),
            P("ep", "tp"),
            P("ep", "tp"),
            P("ep", "tp", None, None),
            P("ep", "tp", None, None),
            P("ep"),
            P("tp", None),
            P(),
            P("ep", None),
            P("ep", None, "tp"),
            P("ep", None, "tp"),
            P("ep", "tp", None),
        ),
        out_specs=P(("ep", "tp"), None),
        check_vma=False,
    )
```

profile of v0, /device:TPU:1, one launch (start us, length us, event | category | flops | bytes accessed | tf_op | source)
XLA Modules:
  0.0 230.4 jit_solution(11718140387330859440)
XLA Ops:
  6.5 0.0 copy-start
  6.6 0.9 iota_compare_fusion.2
  7.4 1.0 reshape.301
  8.4 0.9 fusion.67
  9.3 0.0 copy-start.5
  9.3 1.8 fusion.9
  11.2 0.6 fusion.10
  11.9 0.0 copy-done.5
  11.9 0.0 copy-start.3
  11.9 0.7 fusion.38
  12.6 0.0 copy-done.3
  12.6 0.2 fusion.36
  12.9 0.0 copy-start.4
  12.9 0.1 convert_element_type.59
  13.0 0.0 copy-done
  13.1 1.7 convolution_convert_fusion.1
  14.8 5.0 %all-to-all-start = ((bf16[4,16,2880]{2,1,0:T(8,128)(2,1)}), bf16[4,16,2880]{2,1,0:T(8,128)(2,1)S(1)}, u32[]{:S(2)}, u32[]{:S(2)}) async-start(bf16[4,16,2880]{2,1,0:T(8,128)(2,1)} %bitcast.78), calls=%async_computation | async-start | bytes 753664 | tf_op jit(solution)/shard_map/all_to_all | solution.py:14
  19.8 0.0 all-gather.2.cloned.1.call-start
  19.8 0.0 copy-done.4
  19.8 0.1 constant_dynamic-slice_fusion
  19.9 0.1 copy.33
  20.0 0.1 eq.43
  20.1 0.1 fusion.54
  20.1 0.1 reduce_window_sum.11
  20.2 0.2 select_reduce_fusion
  20.4 0.1 reshape.307
  20.5 5.4 %all-to-all-done = bf16[4,16,2880]{2,1,0:T(8,128)(2,1)S(1)} async-done(((bf16[4,16,2880]{2,1,0:T(8,128)(2,1)}), bf16[4,16,2880]{2,1,0:T(8,128)(2,1)S(1)}, u32[]{:S(2)}, u32[]{:S(2)}) %all-to-all-start) | async-done | bytes 368672 | tf_op jit(solution)/shard_map/all_to_all | solution.py:14
  26.0 1.0 multiply_reduce_fusion.1
  27.1 1.0 multiply_convert_fusion
  28.0 0.0 copy-start.1
  28.1 0.6 copy-done.1
  28.7 0.8 broadcast_in_dim.70
  29.5 1.2 reshape.319
  30.7 1.3 broadcast_in_dim.46
  31.9 13.1 %scatter_fusion = bf16[64,2,2880]{2,1,0:T(2,128)(2,1)} fusion(bf16[64,2,2880]{2,1,0:T(2,128)(2,1)} %broadcast_in_dim.46, s32[64]{0:T(128)S(1)} %get-tuple-element.5, bf16[64,2880]{1,0:T(8,128)(2,1)S(1)} %reshape.319), kind=kCustom, calls=%fused_computation.1 | custom fusion | bytes 1106432 | tf_op jit(solution)/shard_map/scatter | solution.py:128
  45.1 36.5 %all_to_all.15 = bf16[64,2,2880]{2,1,0:T(2,128)(2,1)S(1)} all-to-all(bf16[64,2,2880]{2,1,0:T(2,128)(2,1)} %scatter_fusion), channel_id=1, replica_groups=mesh['ep'=64,'tp'=4] {'ep'}, dimensions={0} | all-to-all | bytes 1474560 | tf_op jit(solution)/shard_map/all_to_all | solution.py:131
  81.6 0.9 copy.35
  82.5 0.0 all-gather.2.cloned.1.call-update
  82.5 0.2 reduce-scatter.2.cloned.1.call-start
  82.8 35.4 %all-gather.2.cloned.1.call-done = bf16[64,8,2880]{2,0,1:T(8,128)(2,1)} async-done(((bf16[64,2,2880]{2,0,1:T(8,128)(2,1)}), bf16[64,8,2880]{2,0,1:T(8,128)(2,1)}) %all-gather.2.cloned.1.call-update) | async-done | bytes 2949136 | tf_op jit(solution)/shard_map/all_gather | solution.py:130
  118.2 5.3 %fusion = f32[512,384]{1,0:T(8,128)} fusion(bf16[64,8,2880]{2,0,1:T(8,128)(2,1)} %all-gather.2.cloned.1.call-done, bf16[1,2880,384]{2,1,0:T(8,128)(2,1)} %param.23), kind=kOutput, calls=%fused_computation.4 | convolution fusion | flops 1132462080 | bytes 5947392 | tf_op jit(solution)/shard_map/dot_general | solution.py:69
  123.5 8.7 %convolution_convert_fusion = bf16[64,8,2880]{2,1,0:T(8,128)(2,1)} fusion(bf16[1,384,2880]{1,2,0:T(8,128)(2,1)} %param.25, f32[512,384]{1,0:T(8,128)} %fusion, bf16[1,2880,384]{2,1,0:T(8,128)(2,1)} %param.24, bf16[64,8,2880]{2,0,1:T(8,128)(2,1)} %all-gather.2.cloned.1.call-done), kind=kOutput, calls=%fused_computation.2 | convolution fusion | flops 2267971584 | bytes 11108352 | tf_op jit(solution)/shard_map/dot_general | solution.py:74
  132.2 3.9 %copy.37 = bf16[64,8,2880]{2,0,1:T(8,128)(2,1)} copy(bf16[64,8,2880]{2,1,0:T(8,128)(2,1)} %convolution_convert_fusion) | data formatting | bytes 5898240 | tf_op jit(solution)/shard_map/convert_element_type | solution.py:141
  136.1 0.0 reduce-scatter.2.cloned.1.call-update
  136.2 0.0 copy-start.2
  136.2 40.1 %reduce-scatter.2.cloned.1.call-done = bf16[64,2,2880]{2,0,1:T(8,128)(2,1)} async-done(((bf16[64,8,2880]{2,0,1:T(8,128)(2,1)}), bf16[64,2,2880]{2,0,1:T(8,128)(2,1)}) %reduce-scatter.2.cloned.1.call-update) | async-done | bytes 737296 | tf_op jit(solution)/shard_map/reduce_scatter | solution.py:140
  176.3 2.8 %copy.38 = bf16[64,2,2880]{2,1,0:T(2,128)(2,1)} copy(bf16[64,2,2880]{2,0,1:T(8,128)(2,1)} %reduce-scatter.2.cloned.1.call-done) | data formatting | bytes 1474560 | tf_op jit(solution)/shard_map/reduce_scatter | solution.py:140
  179.1 10.9 %all-to-all-start.2 = ((bf16[64,2,2880]{2,1,0:T(2,128)(2,1)}), bf16[64,2,2880]{2,1,0:T(2,128)(2,1)}, u32[]{:S(2)}, u32[]{:S(2)}) async-start(bf16[64,2,2880]{2,1,0:T(2,128)(2,1)} %copy.38), calls=%async_computation.3 | async-start | bytes 1507328 | tf_op jit(solution)/shard_map/all_to_all | solution.py:143
  190.0 0.0 copy-done.2
  190.0 1.2 fusion.68
  191.1 0.2 select_reduce_fusion.1
  191.4 0.1 copy.32
  191.5 20.8 %all-to-all-done.2 = bf16[64,2,2880]{2,1,0:T(2,128)(2,1)} async-done(((bf16[64,2,2880]{2,1,0:T(2,128)(2,1)}), bf16[64,2,2880]{2,1,0:T(2,128)(2,1)}, u32[]{:S(2)}, u32[]{:S(2)}) %all-to-all-start.2) | async-done | bytes 737312 | tf_op jit(solution)/shard_map/all_to_all | solution.py:143
  212.2 2.8 %convert_element_type.66 = f32[64,2,2880]{2,1,0:T(2,128)} convert(bf16[64,2,2880]{2,1,0:T(2,128)(2,1)} %all-to-all-done.2) | non-fusion elementwise | flops 368640 | bytes 2211840 | tf_op jit(solution)/shard_map/convert_element_type | solution.py:145
  215.0 3.1 %gather_fusion = f32[64,2880]{1,0:T(8,128)} fusion(f32[64,2,2880]{2,1,0:T(2,128)} %convert_element_type.66, s32[64]{0:T(128)S(1)} %bitcast.77), kind=kCustom, calls=%fused_computation | custom fusion | bytes 1475072 | tf_op jit(solution)/shard_map/gather | solution.py:146
  218.1 2.2 reshape.310
  220.3 1.7 multiply_reduce_fusion
  222.0 1.6 add_convert_fusion
  (10 shorter events, 0.1 us)
Async XLA Ops:
  6.5 6.5 %copy-start = (bf16[512,2880]{0,1:T(8,128)(2,1)S(1)}, bf16[512,2880]{0,1:T(8,128)(2,1)}, u32[]{:S(2)}) copy-start(bf16[512,2880]{0,1:T(8,128)(2,1)} %param.20) | copy-start | bytes 8847364
  9.3 2.5 %copy-start.5 = (bf16[8,1,64,1024]{3,2,1,0:T(8,128)(2,1)S(1)}, bf16[8,1,64,1024]{3,2,1,0:T(8,128)(2,1)}, u32[]{:S(2)}) copy-start(bf16[8,1,64,1024]{3,2,1,0:T(8,128)(2,1)} %param.18) | copy-start | bytes 3145732
  11.9 0.8 copy-start.3
  12.9 6.9 %copy-start.4 = (s32[64,4]{0,1:T(4,128)S(1)}, s32[64,4]{0,1:T(4,128)}, u32[]{:S(2)}) copy-start(s32[64,4]{0,1:T(4,128)} %param.22) | copy-start | bytes 3076
  14.8 11.2 %all-to-all-start = ((bf16[4,16,2880]{2,1,0:T(8,128)(2,1)}), bf16[4,16,2880]{2,1,0:T(8,128)(2,1)S(1)}, u32[]{:S(2)}, u32[]{:S(2)}) async-start(bf16[4,16,2880]{2,1,0:T(8,128)(2,1)} %bitcast.78), calls=%async_computation | async-start | bytes 753664 | tf_op jit(solution)/shard_map/all_to_all | solution.py:14
  19.8 98.4 %all-gather.2.cloned.1.call-start = ((), (), s32[]{:S(2)}) async-start(), calls=%async_computation.4 | async-start | bytes 3768320 | tf_op jit(solution)/shard_map/all_gather | solution.py:130
  28.0 0.6 copy-start.1
  82.5 93.8 %reduce-scatter.2.cloned.1.call-start = ((), (), s32[]{:S(2)}) async-start(), calls=%async_computation.5 | async-start | bytes 3768320 | tf_op jit(solution)/shard_map/reduce_scatter | solution.py:140
  136.2 53.8 %copy-start.2 = (bf16[16,2880]{1,0:T(8,128)(2,1)S(1)}, bf16[16,2880]{1,0:T(8,128)(2,1)}, u32[]{:S(2)}) copy-start(bf16[16,2880]{1,0:T(8,128)(2,1)} %copy-done.1) | copy-start | bytes 276484
  179.1 33.2 %all-to-all-start.2 = ((bf16[64,2,2880]{2,1,0:T(2,128)(2,1)}), bf16[64,2,2880]{2,1,0:T(2,128)(2,1)}, u32[]{:S(2)}, u32[]{:S(2)}) async-start(bf16[64,2,2880]{2,1,0:T(2,128)(2,1)} %copy.38), calls=%async_computation.3 | async-start | bytes 1507328 | tf_op jit(solution)/shard_map/all_to_all | solution.py:143
Sparse Core Ops, SparseCore 0:
  82.7 35.4 all-gather.1
  136.3 39.9 reduce-scatter.1
where the time goes:
time: 231 us; the launch traced here: 230 us
  waiting for transfers between devices  102 us (44%)
  blocking collectives  36.5 us (16%)
  local copies, waits for them, and re-layouts  31.4 us (14%)
  matrix products  20.7 us (9%)
  starting transfers between devices  16.1 us (7%)
  between operations  13.6 us (6%)
  other arithmetic  10.2 us (4%)
    reduce_scatter x1, waiting for transfers between devices, body(): lax.psum_scatter(grouped.astype(jnp.bfloat16), 'tp', scatter_dimension=1,...  40.1 us
    all_to_all x1, blocking collectives, body(): lax.all_to_all(outgoing, 'ep', split_axis=0, concat_axis=0, tiled=True)  36.5 us
    all_gather x1, waiting for transfers between devices, body(): lax.all_gather(lax.all_to_all(outgoing, 'ep', split_axis=0, concat_axis=0...  35.4 us
    all_to_all x1, waiting for transfers between devices, body(): lax.all_to_all(group_total.astype(jnp.bfloat16), 'ep', split_axis=0, conc...  20.8 us
    scatter x1, local copies, waits for them, and re-layouts, body(): outgoing.at[flat_routes, slot_index]  13.1 us
    all_to_all x1, starting transfers between devices, body(): lax.all_to_all(group_total.astype(jnp.bfloat16), 'ep', split_axis=0, conc...  10.9 us
    dot_general x1, matrix products, expert_apply(): jnp.dot(activated, w_down[0], preferred_element_type=jnp.float32)  8.75 us
    all_to_all x1, waiting for transfers between devices, sent_and_summed(): lax.all_to_all(parts, axis, split_axis=0, concat_axis=0, tiled=True)  5.44 us
  transfers between devices with their start and end apart: 4, of which 4 were waited for; matrix products, arithmetic and copies ran while one was open for 1% of the time, Pallas kernels for 0%

commit v1 on v0

v1 whole, which is shorter than its diff:
```python
import jax
import jax.numpy as jnp
from jax import lax
from jax.experimental import pallas as pl
from jax.experimental.pallas import tpu as pltpu
from jax.sharding import PartitionSpec as P

MESH = pl.DeviceIdType.MESH
NZ, NX, NC, NY = 8, 4, 2, 4
NXC = NX * NC
D = 2880
FF = 384
ROWS = 16
SLOTS = 128
WIDTHS = (512, 512, 512, 512, 512, 320)
STARTS = tuple(sum(WIDTHS[:i]) for i in range(len(WIDTHS)))
C = len(WIDTHS)
BF = jnp.bfloat16
F32 = jnp.float32


def attend(queries, new_keys, new_values, key_cache, value_cache, cache_lengths):
    seq_count, kv_count, head_dim, length = key_cache.shape
    new_count = queries.shape[0] // seq_count
    group_size = queries.shape[1] // (kv_count * head_dim)
    row_count = new_count * group_size
    scale = head_dim ** (-0.5)
    query_block = queries.reshape(seq_count, new_count, kv_count, group_size, head_dim)
    query_block = query_block.transpose(0, 2, 1, 3, 4).reshape(
        seq_count, kv_count, row_count, head_dim
    )
    fresh_keys = new_keys.reshape(seq_count, new_count, kv_count, head_dim).transpose(0, 2, 1, 3)
    fresh_values = new_values.reshape(seq_count, new_count, kv_count, head_dim).transpose(
        0, 2, 1, 3
    )
    cache_scores = (
        jnp.einsum("skrd,skdl->skrl", query_block, key_cache, preferred_element_type=jnp.float32)
        * scale
    )
    in_cache = jnp.arange(length)[None, :] < cache_lengths[:, None]
    cache_scores = jnp.where(in_cache[:, None, None, :], cache_scores, -1e30)
    fresh_scores = (
        jnp.einsum("skrd,sknd->skrn", query_block, fresh_keys, preferred_element_type=jnp.float32)
        * scale
    )
    causal = (jnp.arange(row_count) // group_size)[:, None] >= jnp.arange(new_count)[None, :]
    fresh_scores = jnp.where(causal[None, None, :, :], fresh_scores, -1e30)
    row_max = jnp.maximum(
        jnp.max(cache_scores, -1, keepdims=True), jnp.max(fresh_scores, -1, keepdims=True)
    )
    cache_exp = jnp.exp(cache_scores - row_max)
    fresh_exp = jnp.exp(fresh_scores - row_max)
    denom_sum = jnp.sum(cache_exp, -1, keepdims=True) + jnp.sum(fresh_exp, -1, keepdims=True)
    cache_probs = (cache_exp / denom_sum).astype(jnp.bfloat16)
    fresh_probs = (fresh_exp / denom_sum).astype(jnp.bfloat16)
    head_mix = jnp.einsum(
        "skrl,skdl->skrd", cache_probs, value_cache, preferred_element_type=jnp.float32
    )
    head_mix = head_mix + jnp.einsum(
        "skrn,sknd->skrd", fresh_probs, fresh_values, preferred_element_type=jnp.float32
    )
    head_mix = head_mix.reshape(seq_count, kv_count, new_count, group_size, head_dim).transpose(
        0, 2, 1, 3, 4
    )
    return head_mix.reshape(seq_count * new_count, kv_count * group_size * head_dim).astype(
        jnp.bfloat16
    )


def moe_kernel(
    part, hid, routes, wr_h, wg_h, wu_h, wd_h, out,
    wr, wgu, wd, r0, res, zs, zr, xs, xa, acc, act, po, ra, rb, xs2, xr2, zs2, zr2,
    w_sem, s0s, s0r, zss, zsr, xss, xsr, yss, ysr, ras, rar, rbs, rbr, x2s, x2r, z2s, z2r,
):
    ep = lax.axis_index("ep")
    y = lax.axis_index("tp")
    c = ep % NC
    x = (ep // NC) % NX
    z = ep // NXC
    xc = x * NC + c

    wcp = [
        pltpu.make_async_copy(wr_h, wr, w_sem.at[0]),
        pltpu.make_async_copy(wg_h.at[0], wgu.at[:, pl.ds(0, FF)], w_sem.at[1]),
        pltpu.make_async_copy(wu_h.at[0], wgu.at[:, pl.ds(FF, FF)], w_sem.at[2]),
        pltpu.make_async_copy(wd_h.at[0], wd, w_sem.at[3]),
    ]
    for cp in wcp:
        cp.start()

    def zdev(j):
        return (((z + j) % NZ) * NXC + xc, y)

    def xidx(jx, jc):
        return ((x + jx) % NX) * NC + (c + jc) % NC

    def xdev(jx, jc):
        return (z * NXC + xidx(jx, jc), y)

    def ydev(d):
        return (ep, (y + d) % NY)

    XJ = [(i // NC, i % NC) for i in range(1, NXC)]

    barrier = pltpu.get_barrier_semaphore()
    peers = [zdev(j) for j in range(1, NZ)] + [xdev(*j) for j in XJ] + [ydev(d) for d in range(1, NY)]
    for dev in peers:
        pl.semaphore_signal(barrier, inc=1, device_id=dev, device_id_type=MESH)
    pl.semaphore_wait(barrier, len(peers))

    def rcopy(src, dst, ssem, rsem, dev):
        cp = pltpu.make_async_remote_copy(
            src_ref=src, dst_ref=dst, send_sem=ssem, recv_sem=rsem,
            device_id=dev, device_id_type=MESH,
        )
        cp.start()
        return cp

    started = []

    c0 = [
        rcopy(part.at[(y + d) % NY], r0.at[d - 1], s0s.at[d - 1], s0r.at[d - 1], ydev(d))
        for d in range(1, NY)
    ]
    started += c0

    rt = routes[y]
    lane = lax.broadcasted_iota(jnp.int32, (ROWS, SLOTS), 1)
    lane_e = lane // 2
    member = jnp.zeros((ROWS, SLOTS), F32)
    for r in range(4):
        member = member + jnp.where(rt[:, r : r + 1] == lane_e, 1.0, 0.0)
    ti = lax.broadcasted_iota(jnp.int32, (ROWS, ROWS), 0)
    tj = lax.broadcasted_iota(jnp.int32, (ROWS, ROWS), 1)
    lower = jnp.where(tj < ti, 1.0, 0.0).astype(BF)
    rank = jnp.dot(lower, member.astype(BF), preferred_element_type=F32)
    here = (member > 0.5) & (jnp.abs(rank - (lane % 2).astype(F32)) < 0.5)
    one_hot = jnp.where(here, 1.0, 0.0)
    pick = one_hot.T.astype(BF)

    pr = lax.broadcasted_iota(jnp.int32, (SLOTS, SLOTS), 0)
    pc = lax.broadcasted_iota(jnp.int32, (SLOTS, SLOTS), 1)
    to_x = jnp.where(pc == ((pr // 2) % 8) * 16 + (pr // 16) * 2 + pr % 2, 1.0, 0.0).astype(BF)

    for cp in c0:
        cp.wait_recv()
    resid = hid[y].astype(F32) + (
        part[y].astype(F32) + r0[0].astype(F32) + r0[1].astype(F32) + r0[2].astype(F32)
    )
    res[...] = resid
    normed = (
        resid * lax.rsqrt(jnp.mean(resid * resid, -1, keepdims=True) + 1e-05)
    ).astype(BF)

    cz = []
    for k in range(C):
        w = WIDTHS[k]
        rows = jnp.dot(pick, normed[:, STARTS[k] : STARTS[k] + w], preferred_element_type=F32)
        zs[k][...] = rows.astype(BF).reshape(NZ, ROWS, w)
        cz.append([
            rcopy(zs[k].at[(z + j) % NZ], zr[k].at[j], zss.at[k, j - 1], zsr.at[k, j - 1], zdev(j))
            for j in range(1, NZ)
        ])
        started += cz[k]
        zr[k][0] = zs[k][z]

    wcp[0].wait()
    logits = jnp.dot(normed, wr[...], preferred_element_type=F32)
    le = lax.broadcasted_iota(jnp.int32, (64, SLOTS), 0)
    ls = lax.broadcasted_iota(jnp.int32, (64, SLOTS), 1)
    spread = jnp.where(le == ls // 2, 1.0, 0.0)
    logits = jnp.dot(logits, spread, preferred_element_type=F32, precision=lax.Precision.HIGHEST)
    picked = jnp.where(here, jnp.exp(logits), 0.0)
    weight = picked / jnp.sum(picked, -1, keepdims=True)
    w_hi = weight.astype(BF)
    w_lo = (weight - w_hi.astype(F32)).astype(BF)

    wcp[1].wait()
    wcp[2].wait()
    wcp[3].wait()

    cx, cy, cf = [None] * C, [None] * C, [None] * C

    def stage_x(k):
        w = WIDTHS[k]
        for cp in cz[k]:
            cp.wait_recv()
        rows = jnp.dot(to_x, zr[k][...].reshape(SLOTS, w), preferred_element_type=F32)
        xs[k][...] = rows.astype(BF).reshape(NXC, ROWS, w)
        cx[k] = [
            rcopy(
                xs[k].at[xidx(jx, jc)], xa[k].at[0, jx * NC + jc],
                xss.at[k, jx * NC + jc - 1], xsr.at[k, jx * NC + jc - 1], xdev(jx, jc),
            )
            for jx, jc in XJ
        ]
        started.extend(cx[k])
        xa[k][0, 0] = xs[k][xc]

    def stage_y(k):
        for cp in cx[k]:
            cp.wait_recv()
        cy[k] = [
            rcopy(xa[k].at[0], xa[k].at[1], yss.at[k, 0], ysr.at[k, 0], ydev(1)),
            rcopy(xa[k].at[0], xa[k].at[3], yss.at[k, 1], ysr.at[k, 1], ydev(3)),
        ]
        started.extend(cy[k])

    def stage_f(k):
        lo, hi = pl.ds(0, NXC // 2), pl.ds(NXC // 2, NXC // 2)
        cy[k][0].wait_recv()
        a = rcopy(xa[k].at[1, lo], xa[k].at[2, lo], yss.at[k, 2], ysr.at[k, 2], ydev(1))
        cy[k][1].wait_recv()
        b = rcopy(xa[k].at[3, hi], xa[k].at[2, hi], yss.at[k, 3], ysr.at[k, 3], ydev(3))
        cf[k] = [a, b]
        started.extend(cf[k])

    def stage_m(k):
        w = WIDTHS[k]
        for cp in cf[k]:
            cp.wait_recv()
        g = jnp.dot(
            xa[k][...].reshape(NY * SLOTS, w), wgu[pl.ds(STARTS[k], w), :],
            preferred_element_type=F32,
        )
        if k == 0:
            acc[...] = g
        else:
            acc[...] += g

    for k in range(C + 3):
        if k < C:
            stage_x(k)
        if 0 <= k - 1 < C:
            stage_y(k - 1)
        if 0 <= k - 2 < C:
            stage_f(k - 2)
        if 0 <= k - 3 < C:
            stage_m(k - 3)

    gate = acc[:, 0:FF]
    up = acc[:, FF : 2 * FF]
    act[...] = ((up + 1.0) * gate * jax.nn.sigmoid(1.702 * gate)).astype(BF)

    ca, cb, cx2, cz2 = [None] * C, [None] * C, [None] * C, [None] * C
    half = SLOTS // 2
    lo, hi = pl.ds(0, half), pl.ds(half, half)

    def ret_a(k):
        w = WIDTHS[k]
        p = jnp.dot(act[...], wd[:, STARTS[k] : STARTS[k] + w], preferred_element_type=F32)
        po[k][...] = p.astype(BF).reshape(NY, SLOTS, w)
        ca[k] = [
            rcopy(po[k].at[2, lo], ra[k].at[0], ras.at[k, 0], rar.at[k, 0], ydev(1)),
            rcopy(po[k].at[2, hi], ra[k].at[1], ras.at[k, 1], rar.at[k, 1], ydev(3)),
        ]
        started.extend(ca[k])

    def ret_b(k):
        ca[k][0].wait_recv()
        po[k][3, lo] = (po[k][3, lo].astype(F32) + ra[k][0].astype(F32)).astype(BF)
        a = rcopy(po[k].at[3], rb[k].at[0], rbs.at[k, 0], rbr.at[k, 0], ydev(1))
        ca[k][1].wait_recv()
        po[k][1, hi] = (po[k][1, hi].astype(F32) + ra[k][1].astype(F32)).astype(BF)
        b = rcopy(po[k].at[1], rb[k].at[1], rbs.at[k, 1], rbr.at[k, 1], ydev(3))
        cb[k] = [a, b]
        started.extend(cb[k])

    def ret_x(k):
        w = WIDTHS[k]
        for cp in cb[k]:
            cp.wait_recv()
        total = po[k][0].astype(F32) + rb[k][0].astype(F32) + rb[k][1].astype(F32)
        xs2[k][...] = total.astype(BF).reshape(NXC, ROWS, w)
        cx2[k] = [
            rcopy(
                xs2[k].at[jx * NC + jc], xr2[k].at[xc],
                x2s.at[k, jx * NC + jc - 1], x2r.at[k, jx * NC + jc - 1], xdev(NX - jx, NC - jc),
            )
            for jx, jc in XJ
        ]
        started.extend(cx2[k])
        xr2[k][xc] = xs2[k][0]

    def ret_z(k):
        w = WIDTHS[k]
        for cp in cx2[k]:
            cp.wait_recv()
        rows = jnp.dot(to_x, xr2[k][...].reshape(SLOTS, w), preferred_element_type=F32)
        zs2[k][...] = rows.astype(BF).reshape(NZ, ROWS, w)
        cz2[k] = [
            rcopy(
                zs2[k].at[j], zr2[k].at[z], z2s.at[k, j - 1], z2r.at[k, j - 1], zdev(NZ - j)
            )
            for j in range(1, NZ)
        ]
        started.extend(cz2[k])
        zr2[k][z] = zs2[k][0]

    def finish(k):
        w = WIDTHS[k]
        for cp in cz2[k]:
            cp.wait_recv()
        rows = zr2[k][...].reshape(SLOTS, w)
        mix = jnp.dot(w_hi, rows, preferred_element_type=F32) + jnp.dot(
            w_lo, rows, preferred_element_type=F32
        )
        cols = slice(STARTS[k], STARTS[k] + w)
        out[:, cols] = (res[:, cols] + mix).astype(BF)

    for k in range(C + 4):
        if k < C:
            ret_a(k)
        if 0 <= k - 1 < C:
            ret_b(k - 1)
        if 0 <= k - 2 < C:
            ret_x(k - 2)
        if 0 <= k - 3 < C:
            ret_z(k - 3)
        if 0 <= k - 4 < C:
            finish(k - 4)

    for cp in started:
        cp.wait_send()


def moe(part, hid, routes, w_router, w_gate, w_up, w_down):
    vm = pl.BlockSpec(memory_space=pltpu.VMEM)
    hbm = pl.BlockSpec(memory_space=pl.ANY)

    def bufs(*lead):
        return [pltpu.VMEM((*lead, w), BF) for w in WIDTHS]

    dma = pltpu.SemaphoreType.DMA
    return pl.pallas_call(
        moe_kernel,
        out_shape=jax.ShapeDtypeStruct((ROWS, D), BF),
        in_specs=[vm, vm, vm, hbm, hbm, hbm, hbm],
        out_specs=vm,
        scratch_shapes=[
            pltpu.VMEM((D, 64), BF),
            pltpu.VMEM((D, 2 * FF), BF),
            pltpu.VMEM((FF, D), BF),
            pltpu.VMEM((3, ROWS, D), BF),
            pltpu.VMEM((ROWS, D), F32),
            bufs(NZ, ROWS),
            bufs(NZ, ROWS),
            bufs(NXC, ROWS),
            bufs(NY, NXC, ROWS),
            pltpu.VMEM((NY * SLOTS, 2 * FF), F32),
            pltpu.VMEM((NY * SLOTS, FF), BF),
            bufs(NY, SLOTS),
            bufs(2, SLOTS // 2),
            bufs(2, SLOTS),
            bufs(NXC, ROWS),
            bufs(NXC, ROWS),
            bufs(NZ, ROWS),
            bufs(NZ, ROWS),
            dma((4,)),
            dma((3,)), dma((3,)),
            dma((C, 7)), dma((C, 7)),
            dma((C, 7)), dma((C, 7)),
            dma((C, 4)), dma((C, 4)),
            dma((C, 2)), dma((C, 2)),
            dma((C, 2)), dma((C, 2)),
            dma((C, 7)), dma((C, 7)),
            dma((C, 7)), dma((C, 7)),
        ],
        compiler_params=pltpu.CompilerParams(
            collective_id=0, has_side_effects=True, vmem_limit_bytes=56 * 1024 * 1024
        ),
    )(part, hid, routes, w_router, w_gate, w_up, w_down)


def body(
    hidden,
    queries,
    new_keys,
    new_values,
    key_cache,
    value_cache,
    cache_lengths,
    w_out,
    w_router,
    routes,
    w_gate,
    w_up,
    w_down,
):
    attended = attend(queries, new_keys, new_values, key_cache, value_cache, cache_lengths)
    part = jnp.dot(attended, w_out, preferred_element_type=jnp.float32).astype(BF)
    return moe(
        part.reshape(NY, ROWS, D),
        hidden.reshape(NY, ROWS, D),
        routes.reshape(NY, ROWS, 4),
        w_router,
        w_gate,
        w_up,
        w_down,
    )


def solution(mesh):
    return jax.shard_map(
        body,
        mesh=mesh,
        in_specs=(
            P("ep", None),
            P("ep", "tp"),
            P("ep", "tp"),
            P("ep", "tp"),
            P("ep", "tp", None, None),
            P("ep", "tp", None, None),
            P("ep"),
            P("tp", None),
            P(),
            P("ep", None),
            P("ep", None, "tp"),
            P("ep", None, "tp"),
            P("ep", "tp", None),
        ),
        out_specs=P(("ep", "tp"), None),
        check_vma=False,
    )
```

time: 231 us -> 119 us (0.52)
  waiting for transfers between devices: 102 us -> 0 us
  Pallas kernels: 0 us -> 101 us
  blocking collectives: 36.5 us -> 0 us
  local copies, waits for them, and re-layouts: 31.4 us -> 10.4 us
  starting transfers between devices: 16.1 us -> 0 us
  matrix products: 20.7 us -> 5.5 us
  between operations: 13.6 us -> 0.11 us
  other arithmetic: 10.2 us -> 1.54 us
    pallas_call x0 -> x1, Pallas kernels: none -> 101 us  [moe(): pl.pallas_call(moe_kernel, out_shape=jax.ShapeDtypeStruct((ROWS, D), BF),...]
    reduce_scatter x1 -> x0, waiting for transfers between devices: 40.1 us -> none  [body(): lax.psum_scatter(grouped.astype(jnp.bfloat16), 'tp', scatter_dimension=1,...]
    all_to_all x1 -> x0, blocking collectives: 36.5 us -> none  [body(): lax.all_to_all(outgoing, 'ep', split_axis=0, concat_axis=0, tiled=True)]
    all_gather x1 -> x0, waiting for transfers between devices: 35.4 us -> none  [body(): lax.all_gather(lax.all_to_all(outgoing, 'ep', split_axis=0, concat_axis=0...]
    all_to_all x2 -> x0, waiting for transfers between devices: 26.2 us -> none  [the longest x1 20.8 us: body(): lax.all_to_all(group_total.astype(jnp.bfloat16), 'ep', split_axis=0, conc...]
    all_to_all x2 -> x0, starting transfers between devices: 15.9 us -> none  [the longest x1 10.9 us: body(): lax.all_to_all(group_total.astype(jnp.bfloat16), 'ep', split_axis=0, conc...]
    dot_general x4 -> x1, matrix products: 17 us -> 1.78 us  [body(): jnp.dot(attended, w_out, preferred_element_type=jnp.float32).astype(BF)]
    scatter x1 -> x0, local copies, waits for them, and re-layouts: 13.1 us -> none  [body(): outgoing.at[flat_routes, slot_index]]
  transfers between devices with their start and end apart: 4 -> 0, of which waited for: 4 -> 0; matrix products, arithmetic and copies ran while one was open for 1% -> 0% of each run, Pallas kernels for 0% -> 0%
where the time goes in v1:
time: 119 us; the launch traced here: 118 us
  Pallas kernels  101 us (85%)
  local copies, waits for them, and re-layouts  10.4 us (9%)
  matrix products  5.5 us (5%)
  other arithmetic  1.54 us (1%)
    pallas_call x1, Pallas kernels, moe(): pl.pallas_call(moe_kernel, out_shape=jax.ShapeDtypeStruct((ROWS, D), BF),...  101 us
    unnamed x10, local copies, waits for them, and re-layouts  9.26 us

profile of v1, /device:TPU:1, one launch (start us, length us, event | category | flops | bytes accessed | tf_op | source)
XLA Modules:
  0.0 118.4 jit_solution(5933267036906562740)
XLA Ops:
  0.0 0.0 copy-start
  0.0 0.9 iota_compare_fusion
  0.9 1.4 %copy.14 = s32[64,4]{1,0:T(8,128)} copy(s32[64,4]{0,1:T(4,128)} %param.22) | data formatting | bytes 2048 | tf_op args[9]
  2.3 1.0 reshape.137
  3.3 0.9 fusion.16
  4.2 2.1 %copy.15.wr_h = bf16[2880,64]{1,0:T(8,128)(2,1)} copy(bf16[2880,64]{0,1:T(8,128)(2,1)} %param.21) | data formatting | bytes 737280 | tf_op args[8]
  6.3 0.0 copy-start.2
  6.3 1.8 %fusion = (f32[8,64]{1,0:T(8,128)S(1)}, f32[8,64,1024]{2,1,0:T(8,128)S(1)}) fusion(pred[8,1024]{1,0:T(8,128)(4,1)S(1)} %iota_compare_fusion, bf16[8,64,64]{2,1,0:T(8,128)(2,1)S(1)} %reshape.137, bf16[8,1,64,1024]{3,2,1,0:T(8,128)(2,1)} %param.17), kind=kOutput, calls=%fused_computation.4 | convolution fusion | flops 68681216 | bytes 3221504 | tf_op jit(solution)/shard_map/skrd,skdl->skrl/dot_general | solution.py:37
  8.2 0.6 fusion.1
  8.8 0.0 copy-done.2
  8.8 0.0 copy-start.1
  8.9 0.7 fusion.4
  9.6 0.0 copy-done.1
  9.6 0.2 fusion.2
  9.9 0.1 convert_element_type.20
  10.0 0.0 copy-done
  10.0 1.8 %convolution_convert_fusion = bf16[64,2880]{1,0:T(8,128)(2,1)} fusion(bf16[64,512]{1,0:T(8,128)(2,1)S(1)} %convert_element_type.20, bf16[512,2880]{0,1:T(8,128)(2,1)S(1)} %copy-done), kind=kOutput, calls=%fused_computation | convolution fusion | flops 188928000 | bytes 3383296 | tf_op jit(solution)/shard_map/dot_general | solution.py:391
  11.8 4.2 %copy.16.wd_h = bf16[1,384,2880]{2,1,0:T(8,128)(2,1)} copy(bf16[1,384,2880]{1,2,0:T(8,128)(2,1)} %param.25) | data formatting | bytes 4423680 | tf_op args[12]
  16.0 100.9 %shard_map.127 = bf16[16,2880]{1,0:T(8,128)(2,1)} custom-call(bf16[4,16,2880]{2,1,0:T(8,128)(2,1)} %bitcast.23, bf16[4,16,2880]{2,1,0:T(8,128)(2,1)} %bitcast.24, s32[4,16,4]{2,1,0:T(8,128)} %bitcast.25, bf16[2880,64]{1,0:T(8,128)(2,1)} %copy.15.wr_h, bf16[1,2880,384]{2,1,0:T(8,128)(2,1)} %wg_h.1, bf16[1,2880,384]{2,1,0:T(8,128)(2,1)} %wu_h.1, ...), custom_call_target="tpu_custom_call" | custom-call | tf_op jit(solution)/shard_map/pallas_call | solution.py:335
  116.9 1.5 %copy.18 = bf16[16,2880]{1,0:T(8,128)(2,1)} copy(bf16[16,2880]{1,0:T(8,128)(2,1)} %shard_map.127) | data formatting | bytes 184320
  (5 shorter events, 0.0 us)
Async XLA Ops:
  0.0 10.0 %copy-start = (bf16[512,2880]{0,1:T(8,128)(2,1)S(1)}, bf16[512,2880]{0,1:T(8,128)(2,1)}, u32[]{:S(2)}) copy-start(bf16[512,2880]{0,1:T(8,128)(2,1)} %param.20) | copy-start | bytes 8847364
  6.3 2.5 %copy-start.2 = (bf16[8,1,64,1024]{3,2,1,0:T(8,128)(2,1)S(1)}, bf16[8,1,64,1024]{3,2,1,0:T(8,128)(2,1)}, u32[]{:S(2)}) copy-start(bf16[8,1,64,1024]{3,2,1,0:T(8,128)(2,1)} %param.18) | copy-start | bytes 3145732
  8.8 0.8 copy-start.1

commit v2 on v0

v2 whole, which is shorter than its diff:
```python
import jax
import jax.numpy as jnp
from jax import lax
from jax.experimental import pallas as pl
from jax.experimental.pallas import tpu as pltpu
from jax.sharding import PartitionSpec as P

MESH = pl.DeviceIdType.MESH
NZ, NX, NC, NY = 8, 4, 2, 4
NXC = NX * NC
D = 2880
FF = 384
LEN = 1024
ROWS = 16
SLOTS = 128
K = 3
PAD = K * 1024
DP = 2944
CUT = 1536
GROUPS = ((0,), (1, 7), (3, 5), (4,), (2,), (6,))
MULS = ((0, 1), (2, 3), (4, 5))
ORDER = (
    "s0", "s1", "s2", "s3", "s4", "s5", "y0", "y1", "f0", "y2", "y3", "f2",
    "f3", "y4", "y5", "f1", "m1", "a2", "a3", "f4", "f5", "b2", "m0", "a1",
    "b3", "m2", "a4", "a5", "x2", "b1", "a0", "b4", "b5", "x3", "x1", "w0",
    "b0", "x4", "x5", "x0",
)
JZ = tuple(j for g in GROUPS for j in g)
CLASSES = tuple((sum(map(len, GROUPS[:i])), sum(map(len, GROUPS[: i + 1]))) for i in range(len(GROUPS)))
MULS = tuple((m[0], m[-1] + 1) for m in MULS)
BF = jnp.bfloat16
F32 = jnp.float32


def moe_kernel(
    lens, q_h, nk_h, nv_h, hid_h, rt_h, kc_h, vc_h, wo_h, wr_h, wg_h, wu_h, wd_h, out,
    q, nk, nv, hid, routes, sco, prb, kc, vc, wo, part, wr, wgu, wd, r0, res, nrm, zs, xa, xm, po, ra1, ra2, rb, ys, rr,
    met, in_sem, kv_sem, w_sem, s0s, s0r, zss, zsr, yss, ysr, ras, rar, rbs, rbr, xss, xsr,
):
    ep = lax.axis_index("ep")
    y = lax.axis_index("tp")
    c = ep % NC
    x = (ep // NC) % NX
    z = ep // NXC
    xc = x * NC + c

    turns = (2, 1, 3, 0)
    blocks = [(y + d) % NY for d in turns]
    kvcp = []
    for i, b in enumerate(blocks):
        two = pl.ds(b * 2, 2)
        kvcp.append((
            pltpu.make_async_copy(kc_h.at[two, 0], kc.at[i], kv_sem.at[0, i]),
            pltpu.make_async_copy(vc_h.at[two, 0], vc.at[i], kv_sem.at[1, i]),
        ))
    wocp = pltpu.make_async_copy(wo_h, wo, w_sem.at[4])
    wcp = [
        pltpu.make_async_copy(wr_h, wr, w_sem.at[0]),
        pltpu.make_async_copy(wg_h.at[0], wgu.at[:, pl.ds(0, FF)], w_sem.at[1]),
        pltpu.make_async_copy(wu_h.at[0], wgu.at[:, pl.ds(FF, FF)], w_sem.at[2]),
        pltpu.make_async_copy(wd_h.at[0], wd.at[pl.ds(0, D)], w_sem.at[3]),
    ]
    small = [(q_h, q), (nk_h, nk), (nv_h, nv), (rt_h, routes), (hid_h, hid)]
    incp = [pltpu.make_async_copy(a, b, in_sem.at[i]) for i, (a, b) in enumerate(small)]
    incp[0].start()
    for pair in kvcp[:3]:
        pair[0].start()
    for cp in incp[1:3]:
        cp.start()
    for pair in kvcp[:3]:
        pair[1].start()
    wocp.start()
    for cp in kvcp[3]:
        cp.start()
    for cp in incp[3:]:
        cp.start()

    def eidx(jz, i, sign=1):
        jx, jc = sign * (i // NC), i % NC
        return ((z + sign * jz) % NZ) * NXC + ((x + jx) % NX) * NC + (c + jc) % NC

    def ydev(d):
        return (ep, (y + d) % NY)

    FAR = (4, 5, 2, 3, 6, 7, 1, 0)
    PEERS = [(p, i) for p in range(NZ) for i in FAR if (p, i) != (0, 0)]

    barrier = pltpu.get_barrier_semaphore()
    LINES = [(eidx(j, 0), y) for j in range(1, NZ)] + [ydev(d) for d in range(1, NY)]
    CROSS = [(eidx(0, i), y) for i in FAR if i]
    for dev in LINES + CROSS:
        pl.semaphore_signal(barrier, inc=1, device_id=dev, device_id_type=MESH)

    def rcopy(src, dst, ssem, rsem, dev):
        cp = pltpu.make_async_remote_copy(
            src_ref=src, dst_ref=dst, send_sem=ssem, recv_sem=rsem,
            device_id=dev, device_id_type=MESH,
        )
        cp.start()
        return cp

    started = []

    pos = lax.broadcasted_iota(jnp.int32, (64, LEN), 1)
    causal = (
        lax.broadcasted_iota(jnp.int32, (64, 8), 0) % 8
        >= lax.broadcasted_iota(jnp.int32, (64, 8), 1)
    )
    scale = 64 ** (-0.5)

    def attend(which):
        rows = [(i, s) for i in which for s in range(2)]
        fresh, mixes = {}, []
        for i, s in rows:
            if s == 0:
                kvcp[i][0].wait()
            b = blocks[i]
            r = slice(s * 8, s * 8 + 8)
            qb, nkb = q[b].astype(F32), nk[b].astype(F32)
            qs = jnp.concatenate([qb[r, h * 64 : h * 64 + 64] for h in range(8)], 0).astype(BF)
            sc = jnp.dot(qs, kc[i, s], preferred_element_type=F32) * scale
            sco[i * 2 + s] = jnp.where(pos < lens[b * 2 + s], sc, -1e30)
            fs = lax.dot_general(
                qs, nkb[r].astype(BF), (((1,), (1,)), ((), ())), preferred_element_type=F32
            ) * scale
            fresh[i, s] = jnp.where(causal, fs, -1e30)
        for i, s in rows:
            sc, fs = sco[i * 2 + s], fresh[i, s]
            top = jnp.maximum(jnp.max(sc, -1, keepdims=True), jnp.max(fs, -1, keepdims=True))
            se = jnp.exp(sc - top)
            fe = jnp.exp(fs - top)
            inv = 1.0 / (jnp.sum(se, -1, keepdims=True) + jnp.sum(fe, -1, keepdims=True))
            prb[i * 2 + s] = (se * inv).astype(BF)
            fresh[i, s] = (fe * inv).astype(BF)
        for i, s in rows:
            if s == 0:
                kvcp[i][1].wait()
            r = slice(s * 8, s * 8 + 8)
            nvb = nv[blocks[i]].astype(F32)
            mix = lax.dot_general(
                prb[i * 2 + s], vc[i, s], (((1,), (1,)), ((), ())), preferred_element_type=F32
            ) + jnp.dot(fresh[i, s], nvb[r].astype(BF), preferred_element_type=F32)
            mixes.append(jnp.concatenate([mix[h * 8 : h * 8 + 8] for h in range(8)], 1))
        return jnp.concatenate(mixes, 0).astype(BF)

    def project(att):
        return lax.dot_general(
            att, wo[...], (((1,), (1,)), ((), ())), preferred_element_type=F32
        ).astype(BF)

    c0 = []

    def send_part(d):
        c0.append(
            rcopy(part.at[d], r0.at[d - 1], s0s.at[d - 1], s0r.at[d - 1], ydev(d))
        )

    with jax.named_scope("in0"):
        for cp in incp[:3]:
            cp.wait()
    with jax.named_scope("at0"):
        att = attend((0, 1, 2))
        for cp in wcp:
            cp.start()
    with jax.named_scope("wo0"):
        wocp.wait()
        three = project(att)
        for i in range(3):
            part[turns[i]] = three[i * ROWS : (i + 1) * ROWS]
    with jax.named_scope("bar"):
        pl.semaphore_wait(barrier, len(LINES) + len(CROSS))
        for dev in CROSS:
            pl.semaphore_signal(met, inc=1, device_id=dev, device_id_type=MESH)
        for d in turns[:3]:
            send_part(d)
        started += c0
    with jax.named_scope("at2"):
        att = attend((3,))
        for cp in incp[3:]:
            cp.wait()
    with jax.named_scope("wo2"):
        part[0] = project(att)

    own_r = lax.broadcasted_iota(jnp.int32, (ROWS, NY * ROWS), 0) + y * ROWS
    own_c = lax.broadcasted_iota(jnp.int32, (ROWS, NY * ROWS), 1)
    own = jnp.where(own_r == own_c, 1.0, 0.0).astype(BF)
    rt = lax.dot_general(
        own, routes[...].astype(F32).astype(BF), (((1,), (1,)), ((), ())),
        preferred_element_type=F32,
    )
    lane = lax.broadcasted_iota(jnp.int32, (ROWS, SLOTS), 1)
    lane_f = (lane // 2).astype(F32)
    member = jnp.zeros((ROWS, SLOTS), F32)
    for r in range(4):
        member = member + jnp.where(rt[:, r : r + 1] == lane_f, 1.0, 0.0)
    ti = lax.broadcasted_iota(jnp.int32, (ROWS, ROWS), 0)
    tj = lax.broadcasted_iota(jnp.int32, (ROWS, ROWS), 1)
    lower = jnp.where(tj < ti, 1.0, 0.0).astype(BF)
    rank = jnp.dot(lower, member.astype(BF), preferred_element_type=F32)
    here = (member > 0.5) & (jnp.abs(rank - (lane % 2).astype(F32)) < 0.5)
    one_hot = jnp.where(here, 1.0, 0.0)

    er = lax.broadcasted_iota(jnp.int32, (SLOTS, 1024), 0)
    ec = lax.broadcasted_iota(jnp.int32, (SLOTS, 1024), 1)
    expand = jnp.where(er == (ec // 16) * 2 + ec % 2, 1.0, 0.0).astype(BF)
    same_g = er // ROWS == (ec // 2) % 8

    def spread_out(v):
        wide = jnp.dot(v, expand, preferred_element_type=F32)
        return jnp.where(same_g, jnp.concatenate([wide] * 8, 0), 0.0)

    pick = spread_out(one_hot.astype(BF)).T.astype(BF)

    pr = lax.broadcasted_iota(jnp.int32, (SLOTS, SLOTS), 0)
    pc = lax.broadcasted_iota(jnp.int32, (SLOTS, SLOTS), 1)
    swap = jnp.where(pc == ((pr // 2) % 8) * 16 + (pr // 16) * 2 + pr % 2, 1.0, 0.0).astype(BF)
    wd[pl.ds(D, DP - D)] = jnp.zeros((DP - D, FF), BF)

    with jax.named_scope("w0"):
        for cp in c0:
            cp.wait_recv()
    resid = hid[y].astype(F32) + (
        part[0].astype(F32) + r0[0].astype(F32) + r0[1].astype(F32) + r0[2].astype(F32)
    )
    res[...] = resid
    normed = (
        resid * lax.rsqrt(jnp.mean(resid * resid, -1, keepdims=True) + 1e-05)
    ).astype(BF)

    nrm[...] = jnp.concatenate([normed, jnp.zeros((ROWS, PAD - D), BF)], 1)
    for k in range(K):
        tok = jnp.concatenate(
            [nrm[:, k * 1024 + g * 128 : k * 1024 + g * 128 + 128] for g in range(8)], 0
        )
        rows = jnp.dot(pick, tok, preferred_element_type=F32)
        zs[:, k] = rows.astype(BF).reshape(64, ROWS, 128)
    pl.semaphore_wait(met, len(CROSS))
    xa[0, 0, 0] = zs[ep]

    def stage_s(n):
        for p, i in PEERS:
            if CLASSES[n][0] <= p < CLASSES[n][1]:
                e = eidx(JZ[p], i)
                rcopy(zs.at[e], xa.at[0, p, i], zss.at[0], zsr.at[p], (e, y))

    def arrived(sem, n):
        pltpu.make_async_remote_copy(
            src_ref=zs.at[pl.ds(0, n)], dst_ref=rr.at[pl.ds(0, n)], send_sem=zss.at[0],
            recv_sem=sem, device_id=(ep, (y + 1) % NY), device_id_type=MESH,
        ).wait_recv()

    def sent(sem, n):
        pltpu.make_async_remote_copy(
            src_ref=zs.at[pl.ds(0, n)], dst_ref=rr.at[pl.ds(0, n)], send_sem=sem,
            recv_sem=zsr.at[0], device_id=(ep, (y + 1) % NY), device_id_type=MESH,
        ).wait_send()

    def group(p):
        return NXC - 1 if p == 0 else NXC

    late = {}

    def weigh(_):
        wcp[0].wait()
        logits = lax.dot_general(
            nrm[:, 0:D], wr[...], (((1,), (1,)), ((), ())), preferred_element_type=F32
        )
        le = lax.broadcasted_iota(jnp.int32, (64, SLOTS), 0)
        ls = lax.broadcasted_iota(jnp.int32, (64, SLOTS), 1)
        spread = jnp.where(le == ls // 2, 1.0, 0.0)
        logits = jnp.dot(
            logits, spread, preferred_element_type=F32, precision=lax.Precision.HIGHEST
        )
        picked = jnp.where(here, jnp.exp(logits), 0.0)
        weight = picked / jnp.sum(picked, -1, keepdims=True)
        hi = weight.astype(BF)
        late["hi"] = spread_out(hi).astype(BF)
        late["lo"] = spread_out((weight - hi.astype(F32)).astype(BF)).astype(BF)

    cy, cf, ca, cb = {}, {}, {}, {}

    def stage_y(i):
        p0, p1 = CLASSES[i]
        ps = pl.ds(p0, p1 - p0)
        for p in range(p0, p1):
            arrived(zsr.at[p], group(p))
        cy[i] = [
            rcopy(xa.at[0, ps], xa.at[1, ps], yss.at[i, 0], ysr.at[i, 0], ydev(1)),
            rcopy(xa.at[0, ps], xa.at[3, ps], yss.at[i, 1], ysr.at[i, 1], ydev(3)),
        ]
        started.extend(cy[i])

    def stage_f(i):
        p0, p1 = CLASSES[i]
        ps = pl.ds(p0, p1 - p0)
        lo, hi = pl.ds(0, NXC // 2), pl.ds(NXC // 2, NXC // 2)
        cy[i][0].wait_recv()
        a = rcopy(xa.at[1, ps, lo], xa.at[2, ps, lo], yss.at[i, 2], ysr.at[i, 2], ydev(1))
        cy[i][1].wait_recv()
        b = rcopy(xa.at[3, ps, hi], xa.at[2, ps, hi], yss.at[i, 3], ysr.at[i, 3], ydev(3))
        cf[i] = [a, b]
        started.extend(cf[i])

    def stage_m(i):
        i0, i1 = MULS[i]
        p0, p1 = CLASSES[i0][0], CLASSES[i1 - 1][1]
        n = p1 - p0
        for j in range(i0, i1):
            for cp in cf[j]:
                cp.wait_recv()
        while len(wcp) > 1:
            wcp.pop().wait()

        def unfold(d, _):
            for q in range(n):
                blk = jnp.concatenate(
                    [xa[d, p0 + q, :, k].reshape(SLOTS, 128) for k in range(K)], 1
                )
                r = jnp.dot(swap, blk, preferred_element_type=F32).astype(BF)
                for k in range(K):
                    for g in range(8):
                        xm[d, q, :, k * 1024 + g * 128 : k * 1024 + g * 128 + 128] = r[
                            g * ROWS : (g + 1) * ROWS, k * 128 : k * 128 + 128
                        ]
            return 0

        lax.fori_loop(0, NY, unfold, 0)
        rows = xm[:, 0:n, :, 0:D].reshape(NY * n * ROWS, D)
        h = jnp.dot(rows, wgu[...], preferred_element_type=F32)
        gate, up = h[:, 0:FF], h[:, FF : 2 * FF]
        act = ((up + 1.0) * gate * jax.nn.sigmoid(1.702 * gate)).astype(BF)
        o = lax.dot_general(act, wd[...], (((1,), (1,)), ((), ())), preferred_element_type=F32)
        po[:, p0:p1] = o.astype(BF).reshape(NY, n, ROWS, DP)

    lo, hi = pl.ds(0, CUT), pl.ds(CUT, DP - CUT)

    def ret_a(i):
        p0, p1 = CLASSES[i]
        ps = pl.ds(p0, p1 - p0)
        ca[i] = [
            rcopy(po.at[2, ps, :, lo], ra1.at[ps], ras.at[i, 0], rar.at[i, 0], ydev(1)),
            rcopy(po.at[2, ps, :, hi], ra2.at[ps], ras.at[i, 1], rar.at[i, 1], ydev(3)),
        ]
        started.extend(ca[i])

    def ret_b(i):
        p0, p1 = CLASSES[i]
        ps = pl.ds(p0, p1 - p0)
        ca[i][0].wait_recv()
        po[3, ps, :, lo] = (po[3, ps, :, lo].astype(F32) + ra1[ps].astype(F32)).astype(BF)
        a = rcopy(po.at[3, ps], rb.at[0, ps], rbs.at[i, 0], rbr.at[i, 0], ydev(1))
        ca[i][1].wait_recv()
        po[1, ps, :, hi] = (po[1, ps, :, hi].astype(F32) + ra2[ps].astype(F32)).astype(BF)
        b = rcopy(po.at[1, ps], rb.at[1, ps], rbs.at[i, 1], rbr.at[i, 1], ydev(3))
        cb[i] = [a, b]
        started.extend(cb[i])

    def ret_x(i):
        p0, p1 = CLASSES[i]
        for cp in cb[i]:
            cp.wait_recv()
        for p in range(p0, p1):
            tot = (
                po[0, p].astype(F32) + rb[0, p].astype(F32) + rb[1, p].astype(F32)
            ).astype(BF)
            tot = jnp.concatenate([tot, jnp.zeros((ROWS, PAD - DP), BF)], 1)
            blk = jnp.concatenate(
                [
                    jnp.concatenate(
                        [tot[:, k * 1024 + g * 128 : k * 1024 + g * 128 + 128] for g in range(8)], 0
                    )
                    for k in range(K)
                ],
                1,
            )
            r = jnp.dot(swap, blk, preferred_element_type=F32).astype(BF)
            for k in range(K):
                ys[p, :, k] = r[:, k * 128 : k * 128 + 128].reshape(NXC, ROWS, 128)
            for j in FAR:
                if (p, j) != (0, 0):
                    rcopy(
                        ys.at[p, j], rr.at[ep], xss.at[0], xsr.at[p],
                        (eidx(JZ[p], j, -1), y),
                    )
        if p0 == 0:
            rr[ep] = ys[0, 0]

    steps = {"s": stage_s, "y": stage_y, "f": stage_f, "m": stage_m, "w": weigh, "a": ret_a, "b": ret_b, "x": ret_x}
    for step in ORDER:
        with jax.named_scope(f"d{step}"):
            steps[step[0]](int(step[1]))

    with jax.named_scope("wr"):
        for p in range(NZ):
            arrived(xsr.at[p], group(p))
    for k in range(K):
        rows = rr[:, k].reshape(1024, 128)
        mix = jnp.dot(late["hi"], rows, preferred_element_type=F32) + jnp.dot(
            late["lo"], rows, preferred_element_type=F32
        )
        for g in range(8):
            c0_ = k * 1024 + g * 128
            c1_ = min(c0_ + 128, D)
            if c1_ > c0_:
                out[:, c0_:c1_] = (
                    res[:, c0_:c1_] + mix[g * ROWS : (g + 1) * ROWS, 0 : c1_ - c0_]
                )

    sent(zss.at[0], NZ * NXC - 1)
    sent(xss.at[0], NZ * NXC - 1)
    for cp in started:
        cp.wait_send()


def moe(*args):
    vm = pl.BlockSpec(memory_space=pltpu.VMEM)
    hbm = pl.BlockSpec(memory_space=pl.ANY)

    n = len(CLASSES)
    dma = pltpu.SemaphoreType.DMA
    return pl.pallas_call(
        moe_kernel,
        out_shape=jax.ShapeDtypeStruct((ROWS, D), F32),
        in_specs=[pl.BlockSpec(memory_space=pltpu.SMEM)] + [hbm] * 12,
        out_specs=vm,
        scratch_shapes=[
            pltpu.VMEM((NY, ROWS, 512), BF),
            pltpu.VMEM((NY, ROWS, 64), BF),
            pltpu.VMEM((NY, ROWS, 64), BF),
            pltpu.VMEM((NY, ROWS, D), BF),
            pltpu.VMEM((4, NY * ROWS), jnp.int32),
            pltpu.VMEM((8, 64, LEN), F32),
            pltpu.VMEM((8, 64, LEN), BF),
            pltpu.VMEM((NY, 2, 64, LEN), BF),
            pltpu.VMEM((NY, 2, 64, LEN), BF),
            pltpu.VMEM((D, 512), BF),
            pltpu.VMEM((NY, ROWS, D), BF),
            pltpu.VMEM((64, D), BF),
            pltpu.VMEM((D, 2 * FF), BF),
            pltpu.VMEM((DP, FF), BF),
            pltpu.VMEM((3, ROWS, D), BF),
            pltpu.VMEM((ROWS, D), F32),
            pltpu.VMEM((ROWS, PAD), BF),
            pltpu.VMEM((NZ * NXC, K, ROWS, 128), BF),
            pltpu.VMEM((NY, NZ, NXC, K, ROWS, 128), BF),
            pltpu.VMEM((NY, 3, ROWS, PAD), BF),
            pltpu.VMEM((NY, NZ, ROWS, DP), BF),
            pltpu.VMEM((NZ, ROWS, CUT), BF),
            pltpu.VMEM((NZ, ROWS, DP - CUT), BF),
            pltpu.VMEM((2, NZ, ROWS, DP), BF),
            pltpu.VMEM((NZ, NXC, K, ROWS, 128), BF),
            pltpu.VMEM((NZ * NXC, K, ROWS, 128), BF),
            pltpu.SemaphoreType.REGULAR,
            dma((5,)),
            dma((2, NY)),
            dma((5,)),
            dma((3,)), dma((3,)),
            dma((1,)), dma((NZ,)),
            dma((n, 4)), dma((n, 4)),
            dma((n, 2)), dma((n, 2)),
            dma((n, 2)), dma((n, 2)),
            dma((1,)), dma((NZ,)),
        ],
        compiler_params=pltpu.CompilerParams(
            collective_id=0, has_side_effects=True, vmem_limit_bytes=56 * 1024 * 1024
        ),
    )(*args)


def body(
    hidden,
    queries,
    new_keys,
    new_values,
    key_cache,
    value_cache,
    cache_lengths,
    w_out,
    w_router,
    routes,
    w_gate,
    w_up,
    w_down,
):
    return moe(
        cache_lengths,
        queries.reshape(NY, ROWS, 512),
        new_keys.reshape(NY, ROWS, 64),
        new_values.reshape(NY, ROWS, 64),
        hidden.reshape(NY, ROWS, D),
        routes.T,
        key_cache,
        value_cache,
        w_out.T,
        w_router.T,
        w_gate,
        w_up,
        w_down.transpose(0, 2, 1),
    ).astype(BF)


def solution(mesh):
    return jax.shard_map(
        body,
        mesh=mesh,
        in_specs=(
            P("ep", None),
            P("ep", "tp"),
            P("ep", "tp"),
            P("ep", "tp"),
            P("ep", "tp", None, None),
            P("ep", "tp", None, None),
            P("ep"),
            P("tp", None),
            P(),
            P("ep", None),
            P("ep", None, "tp"),
            P("ep", None, "tp"),
            P("ep", "tp", None),
        ),
        out_specs=P(("ep", "tp"), None),
        check_vma=False,
    )
```

time: 231 us -> 87.1 us (0.38)
  waiting for transfers between devices: 102 us -> 0 us
  Pallas kernels: 0 us -> 85.4 us
  blocking collectives: 36.5 us -> 0 us
  local copies, waits for them, and re-layouts: 31.4 us -> 0 us
  matrix products: 20.7 us -> 0 us
  starting transfers between devices: 16.1 us -> 0 us
  between operations: 13.6 us -> 0.01 us
  other arithmetic: 10.2 us -> 1.57 us
    pallas_call x0 -> x1, Pallas kernels: none -> 85.4 us  [moe(): pl.pallas_call(moe_kernel, out_shape=jax.ShapeDtypeStruct((ROWS, D), F32)...]
    reduce_scatter x1 -> x0, waiting for transfers between devices: 40.1 us -> none  [body(): lax.psum_scatter(grouped.astype(jnp.bfloat16), 'tp', scatter_dimension=1,...]
    all_to_all x1 -> x0, blocking collectives: 36.5 us -> none  [body(): lax.all_to_all(outgoing, 'ep', split_axis=0, concat_axis=0, tiled=True)]
    all_gather x1 -> x0, waiting for transfers between devices: 35.4 us -> none  [body(): lax.all_gather(lax.all_to_all(outgoing, 'ep', split_axis=0, concat_axis=0...]
    all_to_all x2 -> x0, waiting for transfers between devices: 26.2 us -> none  [the longest x1 20.8 us: body(): lax.all_to_all(group_total.astype(jnp.bfloat16), 'ep', split_axis=0, conc...]
    dot_general x8 -> x0, matrix products: 20.7 us -> none  [the longest x1 8.75 us: expert_apply(): jnp.dot(activated, w_down[0], preferred_element_type=jnp.float32)]
    all_to_all x2 -> x0, starting transfers between devices: 15.9 us -> none  [the longest x1 10.9 us: body(): lax.all_to_all(group_total.astype(jnp.bfloat16), 'ep', split_axis=0, conc...]
    scatter x1 -> x0, local copies, waits for them, and re-layouts: 13.1 us -> none  [body(): outgoing.at[flat_routes, slot_index]]
  transfers between devices with their start and end apart: 4 -> 0, of which waited for: 4 -> 0; matrix products, arithmetic and copies ran while one was open for 1% -> 0% of each run, Pallas kernels for 0% -> 0%
where the time goes in v2:
time: 87.1 us; the launch traced here: 87 us
  Pallas kernels  85.4 us (98%)
  other arithmetic  1.57 us (2%)
    pallas_call x1, Pallas kernels, moe(): pl.pallas_call(moe_kernel, out_shape=jax.ShapeDtypeStruct((ROWS, D), F32)...  85.4 us

profile of v2, /device:TPU:1, one launch (start us, length us, event | category | flops | bytes accessed | tf_op | source)
XLA Modules:
  0.0 87.0 jit_solution(3760350237309550492)
XLA Ops:
  0.0 85.4 %shard_map.127 = f32[16,2880]{1,0:T(8,128)} custom-call(s32[8]{0:T(128)} %lens.1, bf16[4,16,512]{2,1,0:T(8,128)(2,1)} %bitcast.12, bf16[4,16,64]{2,1,0:T(8,128)(2,1)} %bitcast.13, bf16[4,16,64]{2,1,0:T(8,128)(2,1)} %bitcast.14, bf16[4,16,2880]{2,1,0:T(8,128)(2,1)} %bitcast.10, s32[4,64]{1,0:T(4,128)} %bitcast.15, bf16[8,1,64,1024]{3,2,1,0:T(8,128)(2,1)} %kc_h.1, ...), custom_call_target="tpu_custom_call" | custom-call | tf_op jit(solution)/shard_map/pallas_call | solution.py:421
  85.4 1.6 %convert_element_type.3 = bf16[16,2880]{1,0:T(8,128)(2,1)} convert(f32[16,2880]{1,0:T(8,128)} %shard_map.127) | non-fusion elementwise | flops 46080 | bytes 276480 | tf_op jit(solution)/shard_map/convert_element_type | solution.py:499

commit v3 on v2

--- a/solution.py
+++ b/solution.py
@@ -17,13 +17,14 @@
 PAD = K * 1024
 DP = 2944
 CUT = 1536
-GROUPS = ((0,), (1, 7), (3, 5), (4,), (2,), (6,))
-MULS = ((0, 1), (2, 3), (4, 5))
+GROUPS = ((0,), (1,), (7,), (3,), (5,), (4,), (2,), (6,))
+MULS = ((0, 1, 2), (3, 4), (5, 6, 7))
 ORDER = (
-    "s0", "s1", "s2", "s3", "s4", "s5", "y0", "y1", "f0", "y2", "y3", "f2",
-    "f3", "y4", "y5", "f1", "m1", "a2", "a3", "f4", "f5", "b2", "m0", "a1",
-    "b3", "m2", "a4", "a5", "x2", "b1", "a0", "b4", "b5", "x3", "x1", "w0",
-    "b0", "x4", "x5", "x0",
+    "s4", "s3", "s0", "y0", "s6", "s1", "y4", "s7", "f0", "s5", "y3", "f4",
+    "s2", "y6", "w0", "y1", "f3", "y7", "f6", "y5", "y2", "m1", "a3", "f7",
+    "f5", "a4", "f1", "f2", "b3", "m2", "a6", "a5", "b4", "m0", "a2", "a7",
+    "x3", "b5", "b6", "x4", "a1", "b2", "a0", "x5", "b7", "b1", "x6", "b0",
+    "x2", "x7", "x1", "x0",
 )
 JZ = tuple(j for g in GROUPS for j in g)
 CLASSES = tuple((sum(map(len, GROUPS[:i])), sum(map(len, GROUPS[: i + 1]))) for i in range(len(GROUPS)))
@@ -34,7 +35,7 @@
 
 def moe_kernel(
     lens, q_h, nk_h, nv_h, hid_h, rt_h, kc_h, vc_h, wo_h, wr_h, wg_h, wu_h, wd_h, out,
-    q, nk, nv, hid, routes, sco, prb, kc, vc, wo, part, wr, wgu, wd, r0, res, nrm, zs, xa, xm, po, ra1, ra2, rb, ys, rr,
+    q, nk, nv, hid, routes, sco, prb, kc, vc, wo, part, wr, wgu, wd, r0, res, nrm, zs, xr, xn, po, ra1, ra2, rb, ys, rr,
     met, in_sem, kv_sem, w_sem, s0s, s0r, zss, zsr, yss, ysr, ras, rar, rbs, rbr, xss, xsr,
 ):
     ep = lax.axis_index("ep")
@@ -53,7 +54,7 @@
             pltpu.make_async_copy(kc_h.at[two, 0], kc.at[i], kv_sem.at[0, i]),
             pltpu.make_async_copy(vc_h.at[two, 0], vc.at[i], kv_sem.at[1, i]),
         ))
-    wocp = pltpu.make_async_copy(wo_h, wo, w_sem.at[4])
+    wocp = pltpu.make_async_copy(wo_h, wo.at[pl.ds(0, D)], w_sem.at[4])
     wcp = [
         pltpu.make_async_copy(wr_h, wr, w_sem.at[0]),
         pltpu.make_async_copy(wg_h.at[0], wgu.at[:, pl.ds(0, FF)], w_sem.at[1]),
@@ -143,16 +144,21 @@
             mixes.append(jnp.concatenate([mix[h * 8 : h * 8 + 8] for h in range(8)], 1))
         return jnp.concatenate(mixes, 0).astype(BF)
 
-    def project(att):
+    COLS = [(0, 1024), (1024, 2048), (2048, DP)]
+    wo[pl.ds(D, DP - D)] = jnp.zeros((DP - D, 512), BF)
+
+    def project(att, k):
+        c0, c1 = COLS[k]
         return lax.dot_general(
-            att, wo[...], (((1,), (1,)), ((), ())), preferred_element_type=F32
+            att, wo[pl.ds(c0, c1 - c0)], (((1,), (1,)), ((), ())), preferred_element_type=F32
         ).astype(BF)
 
-    c0 = []
-
-    def send_part(d):
-        c0.append(
-            rcopy(part.at[d], r0.at[d - 1], s0s.at[d - 1], s0r.at[d - 1], ydev(d))
+    c0 = [[] for _ in range(K)]
+
+    def send_part(d, k):
+        cols = pl.ds(COLS[k][0], COLS[k][1] - COLS[k][0])
+        c0[k].append(
+            rcopy(part.at[d, :, cols], r0.at[d - 1, :, cols], s0s.at[d - 1, k], s0r.at[d - 1, k], ydev(d))
         )
 
     with jax.named_scope("in0"):
@@ -162,24 +168,28 @@
         att = attend((0, 1, 2))
         for cp in wcp:
             cp.start()
-    with jax.named_scope("wo0"):
-        wocp.wait()
-        three = project(att)
-        for i in range(3):
-            part[turns[i]] = three[i * ROWS : (i + 1) * ROWS]
-    with jax.named_scope("bar"):
-        pl.semaphore_wait(barrier, len(LINES) + len(CROSS))
-        for dev in CROSS:
-            pl.semaphore_signal(met, inc=1, device_id=dev, device_id_type=MESH)
+    for k in range(K):
+        with jax.named_scope(f"wo{k}"):
+            if k == 0:
+                wocp.wait()
+            three = project(att, k)
+            for i in range(3):
+                part[turns[i], :, COLS[k][0] : COLS[k][1]] = three[i * ROWS : (i + 1) * ROWS]
+        if k == 0:
+            with jax.named_scope("bar"):
+                pl.semaphore_wait(barrier, len(LINES) + len(CROSS))
+                for dev in CROSS:
+                    pl.semaphore_signal(met, inc=1, device_id=dev, device_id_type=MESH)
         for d in turns[:3]:
-            send_part(d)
-        started += c0
+            send_part(d, k)
+        started += c0[k]
     with jax.named_scope("at2"):
         att = attend((3,))
         for cp in incp[3:]:
             cp.wait()
-    with jax.named_scope("wo2"):
-        part[0] = project(att)
+    with jax.named_scope("wo9"):
+        for k in range(K):
+            part[0, :, COLS[k][0] : COLS[k][1]] = project(att, k)
 
     own_r = lax.broadcasted_iota(jnp.int32, (ROWS, NY * ROWS), 0) + y * ROWS
     own_c = lax.broadcasted_iota(jnp.int32, (ROWS, NY * ROWS), 1)
@@ -216,32 +226,46 @@
     swap = jnp.where(pc == ((pr // 2) % 8) * 16 + (pr // 16) * 2 + pr % 2, 1.0, 0.0).astype(BF)
     wd[pl.ds(D, DP - D)] = jnp.zeros((DP - D, FF), BF)
 
-    with jax.named_scope("w0"):
-        for cp in c0:
-            cp.wait_recv()
-    resid = hid[y].astype(F32) + (
-        part[0].astype(F32) + r0[0].astype(F32) + r0[1].astype(F32) + r0[2].astype(F32)
-    )
-    res[...] = resid
-    normed = (
-        resid * lax.rsqrt(jnp.mean(resid * resid, -1, keepdims=True) + 1e-05)
-    ).astype(BF)
-
-    nrm[...] = jnp.concatenate([normed, jnp.zeros((ROWS, PAD - D), BF)], 1)
+    first = [int(st[1]) for st in ORDER[: [st[0] for st in ORDER].index("y")] if st[0] == "s"]
+    pl.semaphore_wait(met, len(CROSS))
+    square = 0.0
     for k in range(K):
+        lo_, hi_ = COLS[k][0], min(COLS[k][1], D)
+        with jax.named_scope(f"w{k}"):
+            for cp in c0[k]:
+                cp.wait_recv()
+        resid = hid[y, :, lo_:hi_].astype(F32) + (
+            part[0, :, lo_:hi_].astype(F32) + r0[0, :, lo_:hi_].astype(F32)
+            + r0[1, :, lo_:hi_].astype(F32) + r0[2, :, lo_:hi_].astype(F32)
+        )
+        res[:, lo_:hi_] = resid
+        square = square + jnp.sum(resid * resid, -1, keepdims=True)
+        if k == K - 1:
+            unit = lax.rsqrt(square / D + 1e-05)
+            unit_hi = unit.astype(BF).astype(F32)
+            spare = lax.broadcasted_iota(jnp.int32, (ROWS, 1024), 1)
+            resid = jnp.concatenate([resid, jnp.zeros((ROWS, PAD - D), F32)], 1)
+            resid = jnp.where(
+                spare == D - lo_, unit_hi, jnp.where(spare == D - lo_ + 1, unit - unit_hi, resid)
+            )
+        nrm[:, k * 1024 : k * 1024 + 1024] = resid.astype(BF)
         tok = jnp.concatenate(
             [nrm[:, k * 1024 + g * 128 : k * 1024 + g * 128 + 128] for g in range(8)], 0
         )
         rows = jnp.dot(pick, tok, preferred_element_type=F32)
         zs[:, k] = rows.astype(BF).reshape(64, ROWS, 128)
-    pl.semaphore_wait(met, len(CROSS))
-    xa[0, 0, 0] = zs[ep]
+        for n in first:
+            for p, i in PEERS:
+                if CLASSES[n][0] <= p < CLASSES[n][1]:
+                    e = eidx(JZ[p], i)
+                    rcopy(zs.at[e, k], xr.at[p, i, k], zss.at[0], zsr.at[p], (e, y))
+    xr[0, 0] = zs[ep]
 
     def stage_s(n):
         for p, i in PEERS:
-            if CLASSES[n][0] <= p < CLASSES[n][1]:
+            if n not in first and CLASSES[n][0] <= p < CLASSES[n][1]:
                 e = eidx(JZ[p], i)
-                rcopy(zs.at[e], xa.at[0, p, i], zss.at[0], zsr.at[p], (e, y))
+                rcopy(zs.at[e], xr.at[p, i], zss.at[0], zsr.at[p], (e, y))
 
     def arrived(sem, n):
         pltpu.make_async_remote_copy(
@@ -264,7 +288,7 @@
         wcp[0].wait()
         logits = lax.dot_general(
             nrm[:, 0:D], wr[...], (((1,), (1,)), ((), ())), preferred_element_type=F32
-        )
+        ) * unit
         le = lax.broadcasted_iota(jnp.int32, (64, SLOTS), 0)
         ls = lax.broadcasted_iota(jnp.int32, (64, SLOTS), 1)
         spread = jnp.where(le == ls // 2, 1.0, 0.0)
@@ -279,25 +303,34 @@
 
     cy, cf, ca, cb = {}, {}, {}, {}
 
+    def tiles():
+        return [(k, g) for k in range(K) for g in range(8) if k * 8 + g < DP // 128]
+
     def stage_y(i):
         p0, p1 = CLASSES[i]
         ps = pl.ds(p0, p1 - p0)
         for p in range(p0, p1):
             arrived(zsr.at[p], group(p))
+            blk = jnp.concatenate([xr[p, :, k].reshape(SLOTS, 128) for k in range(K)], 1)
+            r = jnp.dot(swap, blk, preferred_element_type=F32).astype(BF)
+            for k, g in tiles():
+                t = (k * 8 + g) * 128
+                xn[0, p, :, t : t + 128] = r[g * ROWS : (g + 1) * ROWS, k * 128 : k * 128 + 128]
         cy[i] = [
-            rcopy(xa.at[0, ps], xa.at[1, ps], yss.at[i, 0], ysr.at[i, 0], ydev(1)),
-            rcopy(xa.at[0, ps], xa.at[3, ps], yss.at[i, 1], ysr.at[i, 1], ydev(3)),
+            rcopy(xn.at[0, ps], xn.at[1, ps], yss.at[i, 0], ysr.at[i, 0], ydev(1)),
+            rcopy(xn.at[0, ps], xn.at[3, ps], yss.at[i, 1], ysr.at[i, 1], ydev(3)),
         ]
         started.extend(cy[i])
+
+    lo, hi = pl.ds(0, CUT), pl.ds(CUT, DP - CUT)
 
     def stage_f(i):
         p0, p1 = CLASSES[i]
         ps = pl.ds(p0, p1 - p0)
-        lo, hi = pl.ds(0, NXC // 2), pl.ds(NXC // 2, NXC // 2)
         cy[i][0].wait_recv()
-        a = rcopy(xa.at[1, ps, lo], xa.at[2, ps, lo], yss.at[i, 2], ysr.at[i, 2], ydev(1))
+        a = rcopy(xn.at[1, ps, :, lo], xn.at[2, ps, :, lo], yss.at[i, 2], ysr.at[i, 2], ydev(1))
         cy[i][1].wait_recv()
-        b = rcopy(xa.at[3, ps, hi], xa.at[2, ps, hi], yss.at[i, 3], ysr.at[i, 3], ydev(3))
+        b = rcopy(xn.at[3, ps, :, hi], xn.at[2, ps, :, hi], yss.at[i, 3], ysr.at[i, 3], ydev(3))
         cf[i] = [a, b]
         started.extend(cf[i])
 
@@ -311,28 +344,13 @@
         while len(wcp) > 1:
             wcp.pop().wait()
 
-        def unfold(d, _):
-            for q in range(n):
-                blk = jnp.concatenate(
-                    [xa[d, p0 + q, :, k].reshape(SLOTS, 128) for k in range(K)], 1
-                )
-                r = jnp.dot(swap, blk, preferred_element_type=F32).astype(BF)
-                for k in range(K):
-                    for g in range(8):
-                        xm[d, q, :, k * 1024 + g * 128 : k * 1024 + g * 128 + 128] = r[
-                            g * ROWS : (g + 1) * ROWS, k * 128 : k * 128 + 128
-                        ]
-            return 0
-
-        lax.fori_loop(0, NY, unfold, 0)
-        rows = xm[:, 0:n, :, 0:D].reshape(NY * n * ROWS, D)
-        h = jnp.dot(rows, wgu[...], preferred_element_type=F32)
+        rows = xn[:, p0:p1, :, 0:D].reshape(NY * n * ROWS, D)
+        u = xn[:, p0:p1, :, D:DP].reshape(NY * n * ROWS, DP - D).astype(F32)
+        h = jnp.dot(rows, wgu[...], preferred_element_type=F32) * (u[:, 0:1] + u[:, 1:2])
         gate, up = h[:, 0:FF], h[:, FF : 2 * FF]
         act = ((up + 1.0) * gate * jax.nn.sigmoid(1.702 * gate)).astype(BF)
         o = lax.dot_general(act, wd[...], (((1,), (1,)), ((), ())), preferred_element_type=F32)
         po[:, p0:p1] = o.astype(BF).reshape(NY, n, ROWS, DP)
-
-    lo, hi = pl.ds(0, CUT), pl.ds(CUT, DP - CUT)
 
     def ret_a(i):
         p0, p1 = CLASSES[i]
@@ -433,17 +451,17 @@
             pltpu.VMEM((8, 64, LEN), BF),
             pltpu.VMEM((NY, 2, 64, LEN), BF),
             pltpu.VMEM((NY, 2, 64, LEN), BF),
-            pltpu.VMEM((D, 512), BF),
-            pltpu.VMEM((NY, ROWS, D), BF),
+            pltpu.VMEM((DP, 512), BF),
+            pltpu.VMEM((NY, ROWS, DP), BF),
             pltpu.VMEM((64, D), BF),
             pltpu.VMEM((D, 2 * FF), BF),
             pltpu.VMEM((DP, FF), BF),
-            pltpu.VMEM((3, ROWS, D), BF),
+            pltpu.VMEM((3, ROWS, DP), BF),
             pltpu.VMEM((ROWS, D), F32),
             pltpu.VMEM((ROWS, PAD), BF),
             pltpu.VMEM((NZ * NXC, K, ROWS, 128), BF),
-            pltpu.VMEM((NY, NZ, NXC, K, ROWS, 128), BF),
-            pltpu.VMEM((NY, 3, ROWS, PAD), BF),
+            pltpu.VMEM((NZ, NXC, K, ROWS, 128), BF),
+            pltpu.VMEM((NY, NZ, ROWS, DP), BF),
             pltpu.VMEM((NY, NZ, ROWS, DP), BF),
             pltpu.VMEM((NZ, ROWS, CUT), BF),
             pltpu.VMEM((NZ, ROWS, DP - CUT), BF),
@@ -454,7 +472,7 @@
             dma((5,)),
             dma((2, NY)),
             dma((5,)),
-            dma((3,)), dma((3,)),
+            dma((3, K)), dma((3, K)),
             dma((1,)), dma((NZ,)),
             dma((n, 4)), dma((n, 4)),
             dma((n, 2)), dma((n, 2)),

time: 87.1 us -> 82.9 us (0.952)
  Pallas kernels: 85.4 us -> 81.2 us
    pallas_call x1, Pallas kernels: 85.4 us -> 81.2 us  [moe(): pl.pallas_call(moe_kernel, out_shape=jax.ShapeDtypeStruct((ROWS, D), F32)...]
where the time goes in v3:
time: 82.9 us; the launch traced here: 82.8 us
  Pallas kernels  81.2 us (98%)
  other arithmetic  1.57 us (2%)
    pallas_call x1, Pallas kernels, moe(): pl.pallas_call(moe_kernel, out_shape=jax.ShapeDtypeStruct((ROWS, D), F32)...  81.2 us

profile of v3, /device:TPU:1, one launch (start us, length us, event | category | flops | bytes accessed | tf_op | source)
XLA Modules:
  0.0 82.8 jit_solution(9645539972287754912)
XLA Ops:
  0.0 81.2 %shard_map.127 = f32[16,2880]{1,0:T(8,128)} custom-call(s32[8]{0:T(128)} %lens.1, bf16[4,16,512]{2,1,0:T(8,128)(2,1)} %bitcast.12, bf16[4,16,64]{2,1,0:T(8,128)(2,1)} %bitcast.13, bf16[4,16,64]{2,1,0:T(8,128)(2,1)} %bitcast.14, bf16[4,16,2880]{2,1,0:T(8,128)(2,1)} %bitcast.10, s32[4,64]{1,0:T(4,128)} %bitcast.15, bf16[8,1,64,1024]{3,2,1,0:T(8,128)(2,1)} %kc_h.1, ...), custom_call_target="tpu_custom_call" | custom-call | tf_op jit(solution)/shard_map/pallas_call | solution.py:439
  81.2 1.6 %convert_element_type.3 = bf16[16,2880]{1,0:T(8,128)(2,1)} convert(f32[16,2880]{1,0:T(8,128)} %shard_map.127) | non-fusion elementwise | flops 46080 | bytes 276480 | tf_op jit(solution)/shard_map/convert_element_type | solution.py:517

commit v4 on v3

--- a/solution.py
+++ b/solution.py
@@ -35,7 +35,7 @@
 
 def moe_kernel(
     lens, q_h, nk_h, nv_h, hid_h, rt_h, kc_h, vc_h, wo_h, wr_h, wg_h, wu_h, wd_h, out,
-    q, nk, nv, hid, routes, sco, prb, kc, vc, wo, part, wr, wgu, wd, r0, res, nrm, zs, xr, xn, po, ra1, ra2, rb, ys, rr,
+    q, nk, nv, hid, routes, sco, prb, kc, vc, wo, part, wr, wgu, wd, r0, res, nrm, zs, xr, xn, po, ra1, ra2, rb, ys, rr, wsp,
     met, in_sem, kv_sem, w_sem, s0s, s0r, zss, zsr, yss, ysr, ras, rar, rbs, rbr, xss, xsr,
 ):
     ep = lax.axis_index("ep")
@@ -282,7 +282,6 @@
     def group(p):
         return NXC - 1 if p == 0 else NXC
 
-    late = {}
 
     def weigh(_):
         wcp[0].wait()
@@ -298,8 +297,8 @@
         picked = jnp.where(here, jnp.exp(logits), 0.0)
         weight = picked / jnp.sum(picked, -1, keepdims=True)
         hi = weight.astype(BF)
-        late["hi"] = spread_out(hi).astype(BF)
-        late["lo"] = spread_out((weight - hi.astype(F32)).astype(BF)).astype(BF)
+        wsp[0:SLOTS] = spread_out(hi).astype(BF)
+        wsp[SLOTS:] = spread_out((weight - hi.astype(F32)).astype(BF)).astype(BF)
 
     cy, cf, ca, cb = {}, {}, {}, {}
 
@@ -322,11 +321,14 @@
         ]
         started.extend(cy[i])
 
-    lo, hi = pl.ds(0, CUT), pl.ds(CUT, DP - CUT)
+    def halves(i):
+        both = (pl.ds(0, CUT), pl.ds(CUT, DP - CUT))
+        return both if i % 2 == 0 else both[::-1]
 
     def stage_f(i):
         p0, p1 = CLASSES[i]
         ps = pl.ds(p0, p1 - p0)
+        lo, hi = halves(i)
         cy[i][0].wait_recv()
         a = rcopy(xn.at[1, ps, :, lo], xn.at[2, ps, :, lo], yss.at[i, 2], ysr.at[i, 2], ydev(1))
         cy[i][1].wait_recv()
@@ -355,20 +357,22 @@
     def ret_a(i):
         p0, p1 = CLASSES[i]
         ps = pl.ds(p0, p1 - p0)
+        lo, hi = halves(i)
         ca[i] = [
-            rcopy(po.at[2, ps, :, lo], ra1.at[ps], ras.at[i, 0], rar.at[i, 0], ydev(1)),
-            rcopy(po.at[2, ps, :, hi], ra2.at[ps], ras.at[i, 1], rar.at[i, 1], ydev(3)),
+            rcopy(po.at[2, ps, :, lo], ra1.at[ps, :, lo], ras.at[i, 0], rar.at[i, 0], ydev(1)),
+            rcopy(po.at[2, ps, :, hi], ra2.at[ps, :, hi], ras.at[i, 1], rar.at[i, 1], ydev(3)),
         ]
         started.extend(ca[i])
 
     def ret_b(i):
         p0, p1 = CLASSES[i]
         ps = pl.ds(p0, p1 - p0)
+        lo, hi = halves(i)
         ca[i][0].wait_recv()
-        po[3, ps, :, lo] = (po[3, ps, :, lo].astype(F32) + ra1[ps].astype(F32)).astype(BF)
+        po[3, ps, :, lo] = (po[3, ps, :, lo].astype(F32) + ra1[ps, :, lo].astype(F32)).astype(BF)
         a = rcopy(po.at[3, ps], rb.at[0, ps], rbs.at[i, 0], rbr.at[i, 0], ydev(1))
         ca[i][1].wait_recv()
-        po[1, ps, :, hi] = (po[1, ps, :, hi].astype(F32) + ra2[ps].astype(F32)).astype(BF)
+        po[1, ps, :, hi] = (po[1, ps, :, hi].astype(F32) + ra2[ps, :, hi].astype(F32)).astype(BF)
         b = rcopy(po.at[1, ps], rb.at[1, ps], rbs.at[i, 1], rbr.at[i, 1], ydev(3))
         cb[i] = [a, b]
         started.extend(cb[i])
@@ -408,26 +412,34 @@
         with jax.named_scope(f"d{step}"):
             steps[step[0]](int(step[1]))
 
-    with jax.named_scope("wr"):
-        for p in range(NZ):
-            arrived(xsr.at[p], group(p))
-    for k in range(K):
-        rows = rr[:, k].reshape(1024, 128)
-        mix = jnp.dot(late["hi"], rows, preferred_element_type=F32) + jnp.dot(
-            late["lo"], rows, preferred_element_type=F32
-        )
-        for g in range(8):
-            c0_ = k * 1024 + g * 128
-            c1_ = min(c0_ + 128, D)
-            if c1_ > c0_:
-                out[:, c0_:c1_] = (
-                    res[:, c0_:c1_] + mix[g * ROWS : (g + 1) * ROWS, 0 : c1_ - c0_]
-                )
-
     sent(zss.at[0], NZ * NXC - 1)
-    sent(xss.at[0], NZ * NXC - 1)
     for cp in started:
         cp.wait_send()
+
+    total = jnp.zeros((2 * SLOTS, K * 128), F32)
+    for n in [int(st[1]) for st in ORDER if st[0] == "x"]:
+        for p in range(*CLASSES[n]):
+            with jax.named_scope(f"wr{p}"):
+                arrived(xsr.at[p], group(p))
+            zg = (z + JZ[p]) % NZ
+            got = rr[pl.ds(pl.multiple_of(zg * NXC, NXC), NXC)]
+            blk = jnp.concatenate([got[:, k].reshape(SLOTS, 128) for k in range(K)], 1)
+            total = total + jnp.dot(
+                wsp[:, pl.ds(pl.multiple_of(zg * SLOTS, SLOTS), SLOTS)], blk,
+                preferred_element_type=F32,
+            )
+    mix = total[0:SLOTS] + total[SLOTS:]
+    with jax.named_scope("fin"):
+        for k in range(K):
+            for g in range(8):
+                c0_ = k * 1024 + g * 128
+                c1_ = min(c0_ + 128, D)
+                if c1_ > c0_:
+                    out[:, c0_:c1_] = res[:, c0_:c1_] + mix[
+                        g * ROWS : (g + 1) * ROWS, k * 128 : k * 128 + c1_ - c0_
+                    ]
+
+    sent(xss.at[0], NZ * NXC - 1)
 
 
 def moe(*args):
@@ -463,11 +475,12 @@
             pltpu.VMEM((NZ, NXC, K, ROWS, 128), BF),
             pltpu.VMEM((NY, NZ, ROWS, DP), BF),
             pltpu.VMEM((NY, NZ, ROWS, DP), BF),
-            pltpu.VMEM((NZ, ROWS, CUT), BF),
-            pltpu.VMEM((NZ, ROWS, DP - CUT), BF),
+            pltpu.VMEM((NZ, ROWS, DP), BF),
+            pltpu.VMEM((NZ, ROWS, DP), BF),
             pltpu.VMEM((2, NZ, ROWS, DP), BF),
             pltpu.VMEM((NZ, NXC, K, ROWS, 128), BF),
             pltpu.VMEM((NZ * NXC, K, ROWS, 128), BF),
+            pltpu.VMEM((2 * SLOTS, 1024), BF),
             pltpu.SemaphoreType.REGULAR,
             dma((5,)),
             dma((2, NY)),

time: 82.9 us -> 82.7 us (level)
  no operation moved by 1% of the time
where the time goes in v4:
time: 82.7 us; the launch traced here: 82.6 us
  Pallas kernels  81 us (98%)
  other arithmetic  1.57 us (2%)
    pallas_call x1, Pallas kernels, moe(): pl.pallas_call(moe_kernel, out_shape=jax.ShapeDtypeStruct((ROWS, D), F32)...  81 us

profile of v4, /device:TPU:1, one launch (start us, length us, event | category | flops | bytes accessed | tf_op | source)
XLA Modules:
  0.0 82.6 jit_solution(11893146498295647804)
XLA Ops:
  0.0 81.0 %shard_map.127 = f32[16,2880]{1,0:T(8,128)} custom-call(s32[8]{0:T(128)} %lens.1, bf16[4,16,512]{2,1,0:T(8,128)(2,1)} %bitcast.12, bf16[4,16,64]{2,1,0:T(8,128)(2,1)} %bitcast.13, bf16[4,16,64]{2,1,0:T(8,128)(2,1)} %bitcast.14, bf16[4,16,2880]{2,1,0:T(8,128)(2,1)} %bitcast.10, s32[4,64]{1,0:T(4,128)} %bitcast.15, bf16[8,1,64,1024]{3,2,1,0:T(8,128)(2,1)} %kc_h.1, ...), custom_call_target="tpu_custom_call" | custom-call | tf_op jit(solution)/shard_map/pallas_call | solution.py:451
  81.0 1.6 %convert_element_type.3 = bf16[16,2880]{1,0:T(8,128)(2,1)} convert(f32[16,2880]{1,0:T(8,128)} %shard_map.127) | non-fusion elementwise | flops 46080 | bytes 276480 | tf_op jit(solution)/shard_map/convert_element_type | solution.py:530
